TPU v7x, 128 devices: a whole 4x4x4 slice. The times are simulated.
128 devices in a mesh: chan: 4 (over y), tm: 32 (over z, x, core).
Axes of the slice: x: 4, y: 4, z: 4, core: 2. Of those that a mesh axis runs over, the one named last changes fastest.
Arguments:
- strain: float32 [768, 524288], P('chan', 'tm'), may hold values from -6 to 6
Outputs:
- power: float32 [768, 8192], P('chan', 'tm')
- nyquist: float32 [768], P('chan')
- mean_power: float32 [8192], P('tm')
All inputs are finite; a program needn't handle non-finite values.
Results may differ from a plain program's by a relative error of at most 0.00007.
Values sent between devices are 32-bit elements; how exact they have to be, the bound alone decides.
A program may use at most 192 MiB of HBM per device.

v0:
```python
import functools

import jax
import jax.numpy as jnp
import numpy as np
from jax import lax
from jax.experimental import pallas as pl
from jax.experimental.pallas import tpu as pltpu
from jax.sharding import PartitionSpec as P

ROOT = 128
HALF = ROOT // 2
ROWS = 8


def split_np(table):
    table = table.astype(np.float32)
    high = table.astype(jnp.bfloat16)
    low = (table - high.astype(np.float32)).astype(jnp.bfloat16)
    return high, low


@functools.cache
def tables(tm_count):
    pos = np.arange(ROOT)
    short = 2.0 * np.pi * (np.outer(pos, pos) % ROOT) / ROOT
    cos_s, sin_s = np.cos(short), np.sin(short)
    first = np.concatenate([cos_s[:HALF], -sin_s[:HALF]], axis=0)
    first_hi, first_lo = split_np(first)
    first_all = np.concatenate(
        [
            np.concatenate([first_hi, first_hi], axis=1),
            np.concatenate([first_lo, first_lo], axis=1),
        ],
        axis=0,
    )
    bands = np.arange(HALF).reshape(tm_count, HALF // tm_count)
    order = np.concatenate([bands, ROOT - 1 - bands], axis=1).reshape(-1)
    cos_o, sin_o = cos_s[:, order], sin_s[:, order]
    second = np.concatenate(
        [np.concatenate([cos_o, -sin_o], axis=1), np.concatenate([sin_o, cos_o], axis=1)], axis=0
    )
    second_hi, second_lo = split_np(second)
    second_all = np.concatenate([second_hi, second_hi, second_lo], axis=0)
    long = 2.0 * np.pi * np.outer(np.arange(HALF + ROWS), pos) / (ROOT * ROOT)
    twist = np.concatenate([np.cos(long), np.sin(long)], axis=1).astype(np.float32)
    mirror = np.zeros((2 * ROOT, 2 * ROOT), np.float32)
    for side in range(2):
        for k in range(HALF):
            mirror[side * HALF + k, side * ROOT + k] = 1.0
            if k > 0:
                mirror[ROOT + side * HALF + k, side * ROOT + ROOT - k] = 1.0
    seg_len = ROOT * ROOT
    window = 0.5 - 0.5 * np.cos(2.0 * np.pi * np.arange(seg_len) / seg_len)
    energy = float(np.sum(window * window))
    return first_all, second_all, twist, window.reshape(ROOT, ROOT).astype(np.float32), mirror, energy


def split(value):
    high = value.astype(jnp.bfloat16)
    low = (value - high.astype(jnp.float32)).astype(jnp.bfloat16)
    return high, low


def stage_one(parts, window_ref, first_ref, twist_ref, buf, zbuf, ebuf, row, erow):
    half_len = ROOT * HALF
    total = jnp.zeros((ROWS, ROOT), jnp.float32)
    for ref, offset in parts:
        total = total + jnp.sum(
            jnp.stack([ref[:, offset + ROOT * a : offset + ROOT * (a + 1)] for a in range(HALF)]), axis=0
        )
    mean = jnp.sum(total, axis=1, keepdims=True) * (1.0 / (2 * half_len))
    mean = jnp.broadcast_to(mean, (ROWS, ROOT))
    even = jnp.zeros((ROWS, ROOT), jnp.float32)
    odd = jnp.zeros((ROWS, ROOT), jnp.float32)
    for a in range(ROOT):
        ref, offset = parts[a // HALF]
        start = offset + ROOT * (a % HALF)
        tile = (ref[:, start : start + ROOT] - mean) * window_ref[a : a + 1, :]
        buf[ROWS * a : ROWS * (a + 1), :] = tile
        if a % 2 == 0:
            even = even + tile
        else:
            odd = odd + tile
    alt = even - odd
    sign = (1 - 2 * (lax.broadcasted_iota(jnp.int32, (ROWS, ROOT), 1) % 2)).astype(jnp.float32)
    edge = jnp.sum((even + odd) * sign, axis=1, keepdims=True)
    turn = twist_ref[HALF : HALF + 1, :]
    high, low = split(jnp.concatenate([alt * turn[:, :ROOT], -alt * turn[:, ROOT:]], axis=1))
    ebuf[erow : erow + ROWS, :] = jnp.concatenate([high, low, high], axis=1)
    cos_t, sin_t = twist_ref[:HALF, :ROOT], twist_ref[:HALF, ROOT:]
    for r in range(0, ROWS, 2):
        pair = jnp.concatenate(
            [buf[pl.ds(r, ROOT, stride=ROWS), :], buf[pl.ds(r + 1, ROOT, stride=ROWS), :]], axis=1
        )
        high, low = split(pair)
        out = jnp.dot(
            first_ref[...], jnp.concatenate([high, low], axis=0), preferred_element_type=jnp.float32
        )
        out = out[:ROOT] + out[ROOT:]
        for s in range(2):
            re = out[:HALF, s * ROOT : (s + 1) * ROOT]
            im = out[HALF:, s * ROOT : (s + 1) * ROOT]
            z_hi, z_lo = split(
                jnp.concatenate([re * cos_t + im * sin_t, im * cos_t - re * sin_t], axis=1)
            )
            at = row + (r + s) * HALF
            zbuf[at : at + HALF, 0 : 2 * ROOT] = z_hi
            zbuf[at : at + HALF, 2 * ROOT : 4 * ROOT] = z_lo
            zbuf[at : at + HALF, 4 * ROOT :] = z_hi
    return edge * edge


def squares(left, right):
    out = jnp.dot(left, right, preferred_element_type=jnp.float32)
    return out[:, :ROOT] * out[:, :ROOT] + out[:, ROOT:] * out[:, ROOT:]


def group_sums(lo_ref, hi_ref, right_ref, left_ref, right_on, left_on, per_dev, consts, scratch, put, put_edge):
    window_ref, first_ref, second_ref, twist_ref = consts
    buf, zbuf, ebuf, psum = scratch
    half_len = ROOT * HALF
    block = ROWS * HALF
    lane = lax.broadcasted_iota(jnp.int32, (ROWS, ROOT), 1)
    nyq = []
    for side, own, other, on in ((0, lo_ref, right_ref, right_on), (1, hi_ref, left_ref, left_on)):
        straddle = ((own, half_len), (other, 0)) if side == 0 else ((other, 0), (own, 0))
        first = stage_one(
            ((own, 0), (own, half_len)), window_ref, first_ref, twist_ref, buf, zbuf, ebuf, 0, side * 2 * ROWS
        )
        second = stage_one(
            straddle, window_ref, first_ref, twist_ref, buf, zbuf, ebuf, block, (side * 2 + 1) * ROWS
        )
        nyq.append(first + on * second)
        for r in range(ROWS):
            rows = pl.ds(r * HALF, HALF)
            both = jnp.concatenate([zbuf[rows, :], zbuf[pl.ds(block + r * HALF, HALF), :]], axis=0)
            power = squares(both, second_ref[...])
            psum[r * ROOT + side * HALF : r * ROOT + (side + 1) * HALF, :] = power[:HALF] + on * power[HALF:]
    for r in range(ROWS):
        put(r, jnp.transpose(psum[r * ROOT : (r + 1) * ROOT, :]))
    edge_power = squares(ebuf[...], second_ref[...])
    for side, on in ((0, right_on), (1, left_on)):
        at = side * 2 * ROWS
        mixed = edge_power[at : at + ROWS] + on * edge_power[at + ROWS : at + 2 * ROWS]
        put_edge(side, jnp.where(lane % (2 * per_dev) < per_dev, mixed, jnp.broadcast_to(nyq[side], (ROWS, ROOT))))


def welch_kernel(
    pieces, scale, strain_ref, window_ref, first_ref, second_ref, twist_ref, mirror_ref,
    power_ref, nyquist_ref, mean_ref,
    data, right_half, left_half, sums, edge_rows, edge_sums, from_left, from_right, edge_left, edge_right,
    buf, zbuf, ebuf, psum, channel_sums, channel_from,
    load_sem, halo_send, halo_recv, line_send, line_recv, edge_send, edge_recv, chan_send, chan_recv,
):
    chan, chan_count = lax.axis_index("chan"), lax.axis_size("chan")
    me = lax.axis_index("tm")
    count = lax.axis_size("tm")
    per_dev = HALF // count
    rows = 2 * per_dev
    half_len = ROOT * HALF
    pairs = sums.shape[1]
    groups = pairs // ROWS
    width = pairs // pieces
    has_left, has_right = me > 0, me < count - 1
    right_on, left_on = has_right.astype(jnp.float32), has_left.astype(jnp.float32)

    def block(g, side):
        return pl.ds(pl.multiple_of(side * pairs + g * ROWS, ROWS), ROWS)

    def load(g, side):
        return pltpu.make_async_copy(
            strain_ref.at[block(g, side)], data.at[block(g, side)], load_sem.at[side, g]
        )

    def halo(g, side):
        source = strain_ref.at[block(g, side), pl.ds(side * half_len, half_len)]
        target = (right_half, left_half)[side]
        return pltpu.make_async_remote_copy(
            src_ref=source, dst_ref=target.at[block(g, 0)],
            send_sem=halo_send.at[side, g], recv_sem=halo_recv.at[side, g],
            device_id={"tm": me + (1 if side else -1)}, device_id_type=pl.DeviceIdType.MESH,
        )

    @pl.loop(0, groups)
    def _(g):
        load(g, 0).start()
        load(g, 1).start()

    barrier = pltpu.get_barrier_semaphore()
    for exists, step in ((has_left, -1), (has_right, 1)):
        @pl.when(exists)
        def _():
            pl.semaphore_signal(
                barrier, inc=1, device_id={"tm": me + step}, device_id_type=pl.DeviceIdType.MESH
            )
    for k in range(1, chan_count):
        pl.semaphore_signal(
            barrier, inc=1, device_id={"chan": lax.rem(chan + k, chan_count)},
            device_id_type=pl.DeviceIdType.MESH,
        )
    pl.semaphore_wait(
        barrier, has_left.astype(jnp.int32) + has_right.astype(jnp.int32) + (chan_count - 1)
    )

    @pl.loop(0, groups)
    def _(g):
        for side, exists in ((0, has_left), (1, has_right)):
            @pl.when(exists)
            def _():
                halo(g, side).start()

    edge_rows[...] = jnp.zeros_like(edge_rows)
    for side, exists, ref in ((0, has_right, right_half), (1, has_left, left_half)):
        @pl.when(jnp.logical_not(exists))
        def _():
            ref[...] = jnp.zeros_like(ref)

    def chunk_of(m, side):
        far = lax.rem(m, count - 1)
        return far if side else count - 1 - far

    def sum_part(m, side):
        q = m // (count - 1)
        return sums.at[pl.ds(chunk_of(m, side) * rows, rows), pl.ds(pl.multiple_of(q * width, ROWS), width)]

    def edge_part(m, side):
        return edge_sums.at[pl.ds(chunk_of(m, side) * rows, rows)]

    def line(m, side):
        target = (from_left, from_right)[side]
        return pltpu.make_async_remote_copy(
            src_ref=sum_part(m, side), dst_ref=target.at[m],
            send_sem=line_send.at[side, m], recv_sem=line_recv.at[side, m],
            device_id={"tm": me + (-1 if side else 1)}, device_id_type=pl.DeviceIdType.MESH,
        )

    def edge_line(m, side):
        target = (edge_left, edge_right)[side]
        far = lax.rem(m, count - 1)
        return pltpu.make_async_remote_copy(
            src_ref=edge_part(m, side), dst_ref=target.at[far],
            send_sem=edge_send.at[side, far], recv_sem=edge_recv.at[side, far],
            device_id={"tm": me + (-1 if side else 1)}, device_id_type=pl.DeviceIdType.MESH,
        )

    def take(m, side):
        line(m, side).wait_recv()
        part = sum_part(m, side)
        part[...] = part[...] + (from_left, from_right)[side][m]

        @pl.when(m >= (pieces - 1) * (count - 1))
        def _():
            edge_line(m, side).wait_recv()
            edge = edge_part(m, side)
            edge[...] = edge[...] + (edge_left, edge_right)[side][lax.rem(m, count - 1)]

    messages = (count - 1) * pieces
    hop = 2
    early = max(1, count // 4)

    def place_of(side):
        return count - 1 - me if side else me

    def take_and_send(m, side):
        @pl.when(place_of(side) > 0)
        def _():
            take(m, side)

        line(m, side).start()

        @pl.when(m >= (pieces - 1) * (count - 1))
        def _():
            edge_line(m, side).start()

    @pl.loop(0, groups)
    def _(g):
        load(g, 0).wait()
        load(g, 1).wait()
        for side, exists in ((0, has_right), (1, has_left)):
            @pl.when(exists)
            def _():
                halo(g, side).wait_recv()

        def put(r, value):
            sums[:, g * ROWS + r, :] = value

        def put_edge(side, value):
            edge_rows[block(g, side), :] = value

        group_sums(
            data.at[block(g, 0)], data.at[block(g, 1)], right_half.at[block(g, 0)], left_half.at[block(g, 0)],
            right_on, left_on, per_dev,
            (window_ref, first_ref, second_ref, twist_ref), (buf, zbuf, ebuf, psum), put, put_edge,
        )

        @pl.when(g == groups - 1)
        def _():
            for s in range(edge_sums.shape[1]):
                edge_sums[:, s, :] = jnp.transpose(edge_rows[s * ROOT : (s + 1) * ROOT, :])

        @pl.when(lax.rem(g + 1, groups // pieces) == 0)
        def _():
            q = g // (groups // pieces)
            for side in range(2):
                place = place_of(side)

                @pl.when(place < early)
                def _():
                    @pl.loop(0, count - 1)
                    def _(far):
                        @pl.when(far < count - 1 - place)
                        def _():
                            take_and_send(q * (count - 1) + far, side)

    spread = edge_sums.shape[1]

    @pl.loop(0, messages + hop * (count - 1))
    def _(t):
        for side in range(2):
            place = place_of(side)
            m = t - hop * place

            @pl.when(jnp.logical_and(place >= early, jnp.logical_and(m >= 0, m < messages)))
            def _():
                @pl.when(lax.rem(m, count - 1) < count - 1 - place)
                def _():
                    take_and_send(m, side)

    for side in range(2):
        place = place_of(side)

        @pl.when(place > 0)
        def _():
            @pl.loop(0, pieces)
            def _(q):
                take(q * (count - 1) + (count - 1 - place), side)

    nyquist_ref[...] = edge_sums[me * rows + per_dev] * scale
    for s in range(spread):
        strip = jnp.concatenate(
            [edge_sums[me * rows + j, s : s + 1, :] for j in range(per_dev)]
            + [jnp.zeros((ROOT - per_dev, ROOT), jnp.float32)],
            axis=0,
        )
        edge_rows[s * ROOT : (s + 1) * ROOT, :] = jnp.transpose(strip)
    lanes = lax.broadcasted_iota(jnp.int32, (1, ROOT), 1)
    for j in range(per_dev):
        both = jnp.concatenate([sums[me * rows + j], sums[me * rows + per_dev + j]], axis=1)
        placed = jnp.dot(
            both, mirror_ref[...], precision=lax.Precision.HIGHEST, preferred_element_type=jnp.float32
        )
        factor = jnp.where(jnp.logical_and(lanes == 0, me + j == 0), scale, 2.0 * scale)
        column = jnp.zeros((1, ROOT), jnp.float32)
        for side in range(2):
            middle = edge_rows[side * pairs : (side + 1) * pairs, j : j + 1]
            value = jnp.where(lanes == HALF, middle, placed[:, side * ROOT : (side + 1) * ROOT]) * factor
            power_ref[side * pairs : (side + 1) * pairs, j * ROOT : (j + 1) * ROOT] = value
            column = column + jnp.sum(value, axis=0, keepdims=True)
        channel_sums[j : j + 1, :] = column

    def chan_copy(k):
        return pltpu.make_async_remote_copy(
            src_ref=channel_sums, dst_ref=channel_from.at[k],
            send_sem=chan_send.at[k], recv_sem=chan_recv.at[k],
            device_id={"chan": lax.rem(chan + k, chan_count)}, device_id_type=pl.DeviceIdType.MESH,
        )

    for k in range(1, chan_count):
        chan_copy(k).start()

    @pl.loop(0, groups)
    def _(g):
        for side, exists in ((0, has_left), (1, has_right)):
            @pl.when(exists)
            def _():
                halo(g, side).wait_send()

    @pl.loop(0, messages)
    def _(m):
        for side in range(2):
            place = count - 1 - me if side else me

            @pl.when(lax.rem(m, count - 1) < count - 1 - place)
            def _():
                line(m, side).wait_send()

                @pl.when(m >= (pieces - 1) * (count - 1))
                def _():
                    edge_line(m, side).wait_send()

    channel_from[0] = channel_sums[...]
    for k in range(1, chan_count):
        chan_copy(k).wait()
    total = jnp.zeros_like(channel_sums)
    for source in range(chan_count):
        total = total + channel_from[lax.rem(chan - source + chan_count, chan_count)]
    mean_ref[...] = total * (1.0 / (2 * pairs * chan_count))


def per_device(strain):
    chan_rows, time_width = strain.shape
    seg_len = ROOT * ROOT
    half_len = seg_len // 2
    assert time_width == seg_len and chan_rows % (2 * ROWS) == 0
    tm_count = lax.axis_size("tm")
    segments = 2 * tm_count - 1
    band = half_len // tm_count
    per_dev = HALF // tm_count
    rows = 2 * per_dev
    first_all, second_all, twist, window, mirror, energy = tables(tm_count)
    pairs = chan_rows // 2
    groups = pairs // ROWS
    pieces = 4 if groups % 4 == 0 else 1
    spread = -(-chan_rows // ROOT)
    messages = (tm_count - 1) * pieces
    vmem = pl.BlockSpec(memory_space=pltpu.VMEM)
    f32 = jnp.float32
    power, nyquist, mean_power = pl.pallas_call(
        functools.partial(welch_kernel, pieces, 1.0 / (segments * energy)),
        in_specs=[pl.BlockSpec(memory_space=pl.ANY)] + [vmem] * 5,
        out_specs=[vmem] * 3,
        out_shape=[
            jax.ShapeDtypeStruct((chan_rows, band), f32),
            jax.ShapeDtypeStruct((spread, ROOT), f32),
            jax.ShapeDtypeStruct((per_dev, ROOT), f32),
        ],
        scratch_shapes=[
            pltpu.VMEM((chan_rows, seg_len), f32),
            pltpu.VMEM((pairs, half_len), f32),
            pltpu.VMEM((pairs, half_len), f32),
            pltpu.VMEM((ROOT, pairs, ROOT), f32),
            pltpu.VMEM((spread * ROOT, ROOT), f32),
            pltpu.VMEM((ROOT, spread, ROOT), f32),
            pltpu.VMEM((messages, rows, pairs // pieces, ROOT), f32),
            pltpu.VMEM((messages, rows, pairs // pieces, ROOT), f32),
            pltpu.VMEM((tm_count - 1, rows, spread, ROOT), f32),
            pltpu.VMEM((tm_count - 1, rows, spread, ROOT), f32),
            pltpu.VMEM((ROWS * ROOT, ROOT), f32),
            pltpu.VMEM((2 * ROWS * HALF, 6 * ROOT), jnp.bfloat16),
            pltpu.VMEM((4 * ROWS, 6 * ROOT), jnp.bfloat16),
            pltpu.VMEM((ROWS * ROOT, ROOT), f32),
            pltpu.VMEM((per_dev, ROOT), f32),
            pltpu.VMEM((lax.axis_size("chan"), per_dev, ROOT), f32),
            pltpu.SemaphoreType.DMA((2, groups)),
            pltpu.SemaphoreType.DMA((2, groups)),
            pltpu.SemaphoreType.DMA((2, groups)),
            pltpu.SemaphoreType.DMA((2, messages)),
            pltpu.SemaphoreType.DMA((2, messages)),
            pltpu.SemaphoreType.DMA((2, tm_count - 1)),
            pltpu.SemaphoreType.DMA((2, tm_count - 1)),
            pltpu.SemaphoreType.DMA((lax.axis_size("chan"),)),
            pltpu.SemaphoreType.DMA((lax.axis_size("chan"),)),
        ],
        compiler_params=pltpu.CompilerParams(
            collective_id=0, has_side_effects=True, vmem_limit_bytes=60 * 2**20
        ),
        name="welch",
    )(strain, window, first_all, second_all, twist, mirror)
    return (power, nyquist.reshape(-1)[:chan_rows], mean_power.reshape(-1))


def solution(mesh):
    in_specs = (P("chan", "tm"),)
    out_specs = (P("chan", "tm"), P("chan"), P("tm"))
    return jax.shard_map(
        per_device, mesh=mesh, in_specs=in_specs, out_specs=out_specs, check_vma=False
    )
```

profile of v0, /device:TPU:1, one launch (start us, length us, event | category | flops | bytes accessed | tf_op | source)
XLA Modules:
  0.0 214.9 jit_solution(3176857627206207062)
XLA Ops:
  0.6 210.3 %welch.1 = (f32[192,256]{1,0:T(8,128)}, f32[2,128]{1,0:T(2,128)}, f32[2,128]{1,0:T(2,128)}) custom-call(f32[192,16384]{1,0:T(8,128)} %strain_ref.1, f32[128,128]{1,0:T(8,128)} %constant.10.clone.window_ref, bf16[256,256]{1,0:T(8,128)(2,1)} %constant.11.clone.first_ref, bf16[768,256]{1,0:T(8,128)(2,1)} %constant.12.clone.second_ref, ...), custom_call_target="tpu_custom_call" | custom-call | tf_op jit(solution)/shard_map/welch/pallas_call | solution.py:419
  210.9 1.6 copy.12
  212.5 1.2 copy.13
  213.7 1.2 copy.14
where the time goes:
time: 215 us
  Pallas kernels  210 us (98%)
  local copies, waits for them, and re-layouts  3.99 us (2%)
    pallas_call x1, Pallas kernels, per_device(): pl.pallas_call(functools.partial(welch_kernel, pieces, 1.0 / (segments *...  210 us

commit v1 on v0

v1 whole, which is shorter than its diff:
```python
import functools

import jax
import jax.numpy as jnp
import numpy as np
from jax import lax
from jax.experimental import pallas as pl
from jax.experimental.pallas import tpu as pltpu
from jax.sharding import PartitionSpec as P

ROOT = 128
HALF = ROOT // 2
ROWS = 8


def split_np(table):
    table = table.astype(np.float32)
    high = table.astype(jnp.bfloat16)
    low = (table - high.astype(np.float32)).astype(jnp.bfloat16)
    return high, low


@functools.cache
def tables(tm_count):
    pos = np.arange(ROOT)
    short = 2.0 * np.pi * (np.outer(pos, pos) % ROOT) / ROOT
    cos_s, sin_s = np.cos(short), np.sin(short)
    first = np.concatenate([cos_s[:HALF], -sin_s[:HALF]], axis=0)
    first_hi, first_lo = split_np(first)
    first_all = np.concatenate(
        [
            np.concatenate([first_hi, first_hi], axis=1),
            np.concatenate([first_lo, first_lo], axis=1),
        ],
        axis=0,
    )
    bands = np.arange(HALF).reshape(tm_count, HALF // tm_count)
    order = np.concatenate([bands, ROOT - 1 - bands], axis=1).reshape(-1)
    cos_o, sin_o = cos_s[:, order], sin_s[:, order]
    second = np.concatenate(
        [np.concatenate([cos_o, -sin_o], axis=1), np.concatenate([sin_o, cos_o], axis=1)], axis=0
    )
    second_hi, second_lo = split_np(second)
    second_all = np.concatenate([second_hi, second_hi, second_lo], axis=0)
    long = 2.0 * np.pi * np.outer(np.arange(HALF + ROWS), pos) / (ROOT * ROOT)
    twist = np.concatenate([np.cos(long), np.sin(long)], axis=1).astype(np.float32)
    mirror = np.zeros((2 * ROOT, 2 * ROOT), np.float32)
    for side in range(2):
        for k in range(HALF):
            mirror[side * HALF + k, side * ROOT + k] = 1.0
            mirror[ROOT + side * HALF + k, side * ROOT + (ROOT - k if k else HALF)] = 1.0
    seg_len = ROOT * ROOT
    window = 0.5 - 0.5 * np.cos(2.0 * np.pi * np.arange(seg_len) / seg_len)
    energy = float(np.sum(window * window))
    return first_all, second_all, twist, window.reshape(ROOT, ROOT).astype(np.float32), mirror, energy


def split(value):
    high = value.astype(jnp.bfloat16)
    low = (value - high.astype(jnp.float32)).astype(jnp.bfloat16)
    return high, low


SPAN = 4
CORES = 2


def half_sum(ref, offset):
    parts = [ref[:, offset + ROOT * a : offset + ROOT * (a + 1)] for a in range(HALF)]
    while len(parts) > 1:
        parts = [parts[n] + parts[n + 1] for n in range(0, len(parts), 2)]
    return jnp.sum(parts[0], axis=1, keepdims=True)


def stage_one(parts, mean, consts, buf, zbuf, ebuf, seg, segs, erow):
    window_ref, first_ref, _, twist_ref = consts
    mean = jnp.broadcast_to(mean, (ROWS, ROOT))
    even = jnp.zeros((ROWS, ROOT), jnp.float32)
    odd = jnp.zeros((ROWS, ROOT), jnp.float32)
    for a in range(ROOT):
        ref, offset = parts[a // HALF]
        start = offset + ROOT * (a % HALF)
        tile = (ref[:, start : start + ROOT] - mean) * window_ref[a : a + 1, :]
        buf[ROWS * a : ROWS * (a + 1), :] = tile
        if a % 2 == 0:
            even = even + tile
        else:
            odd = odd + tile
    alt = even - odd
    sign = (1 - 2 * (lax.broadcasted_iota(jnp.int32, (ROWS, ROOT), 1) % 2)).astype(jnp.float32)
    edge = jnp.sum((even + odd) * sign, axis=1, keepdims=True)
    turn = twist_ref[HALF : HALF + 1, :]
    high, low = split(jnp.concatenate([alt * turn[:, :ROOT], -alt * turn[:, ROOT:]], axis=1))
    ebuf[erow : erow + ROWS, :] = jnp.concatenate([high, low, high], axis=1)
    cos_t, sin_t = twist_ref[:HALF, :ROOT], twist_ref[:HALF, ROOT:]
    for r in range(0, ROWS, 2):
        pair = jnp.concatenate(
            [buf[pl.ds(r, ROOT, stride=ROWS), :], buf[pl.ds(r + 1, ROOT, stride=ROWS), :]], axis=1
        )
        high, low = split(pair)
        out = jnp.dot(
            first_ref[...], jnp.concatenate([high, low], axis=0), preferred_element_type=jnp.float32
        )
        out = out[:ROOT] + out[ROOT:]
        for s in range(2):
            re = out[:HALF, s * ROOT : (s + 1) * ROOT]
            im = out[HALF:, s * ROOT : (s + 1) * ROOT]
            z_hi, z_lo = split(
                jnp.concatenate([re * cos_t + im * sin_t, im * cos_t - re * sin_t], axis=1)
            )
            at = ((r + s) * segs + seg) * HALF
            zbuf[at : at + HALF, 0 : 2 * ROOT] = z_hi
            zbuf[at : at + HALF, 2 * ROOT :] = z_lo
    return edge * edge


def squares(left, right):
    out = jnp.dot(left, right, preferred_element_type=jnp.float32)
    return out[:, :ROOT] * out[:, :ROOT] + out[:, ROOT:] * out[:, ROOT:]


def side_sums(side, own, halo, on, wait_halo, consts, scratch):
    second_ref = consts[2]
    buf, zbuf, ebuf, psum = scratch
    half_len = ROOT * HALF
    segs = 2 * CORES
    lane = lax.broadcasted_iota(jnp.int32, (ROWS, ROOT), 1)
    pieces = [(own, half_len * h) for h in range(segs)]
    totals = [half_sum(*piece) for piece in pieces]
    inverse = 1.0 / (2 * half_len)
    nyq = jnp.zeros((ROWS, 1), jnp.float32)
    for seg in range(segs - 1):
        nyq = nyq + stage_one(
            (pieces[seg], pieces[seg + 1]), (totals[seg] + totals[seg + 1]) * inverse,
            consts, buf, zbuf, ebuf, seg, segs, seg * ROWS,
        )
    wait_halo()
    far = (halo, 0)
    straddle = (pieces[-1], far) if side == 0 else (far, pieces[0])
    near = totals[-1] if side == 0 else totals[0]
    nyq = nyq + on * stage_one(
        straddle, (near + half_sum(*far)) * inverse, consts, buf, zbuf, ebuf, segs - 1, segs, (segs - 1) * ROWS
    )

    def fold(power, rows):
        total = power[:rows]
        for seg in range(1, segs - 1):
            total = total + power[seg * rows : (seg + 1) * rows]
        return total + on * power[(segs - 1) * rows :]

    for r in range(ROWS):
        rows = slice(r * segs * HALF, (r + 1) * segs * HALF)
        left = jnp.concatenate([zbuf[rows, :], zbuf[rows, : 2 * ROOT]], axis=1)
        at = r * ROOT + side * HALF
        psum[at : at + HALF, :] = fold(squares(left, second_ref[...]), HALF)
    mixed = fold(squares(ebuf[...], second_ref[...]), ROWS)
    first_rows = pl.ds(side * HALF, ROWS, stride=ROOT)
    psum[first_rows, :] = jnp.where(lane % SPAN >= SPAN // 2, mixed, psum[first_rows, :])
    return nyq


def welch_kernel(
    scale, strain_ref, window_ref, first_ref, second_ref, twist_ref, mirror_ref,
    power_ref, nyquist_ref, mean_ref,
    data, halo, sums, fin, from_partner, z_in, x_in, nyq_rows, nyq_out, nyq_in, nyq_partner,
    buf, zbuf, ebuf, psum, channel_sums, channel_from,
    load_sem, swap_send, swap_recv, halo_send, halo_recv,
    z_send, z_recv, x_send, x_recv, core_send, core_recv,
    nyq_send, nyq_recv, nyq_core_send, nyq_core_recv, chan_send, chan_recv,
):
    chan, chan_count = lax.axis_index("chan"), lax.axis_size("chan")
    me = lax.axis_index("tm")
    core = lax.rem(me, CORES)
    chip = me // CORES
    chips = lax.axis_size("tm") // CORES
    z, x = chip // SPAN, lax.rem(chip, SPAN)
    half_len = ROOT * HALF
    block_len = 2 * half_len
    mine = data.shape[0]
    wide = 2 * ROWS
    steps = mine // wide
    has_left, has_right = chip > 0, chip < chips - 1
    exists = (has_right, has_left)
    on = [flag.astype(jnp.float32) for flag in exists]

    def device(chip_index, core_index):
        return {"tm": chip_index * CORES + core_index}

    def z_peer(step):
        return device(lax.rem(z + step + SPAN, SPAN) * SPAN + x, core)

    def x_peer(step):
        return device(z * SPAN + lax.rem(x + step + SPAN, SPAN), core)

    partner = device(chip, 1 - core)

    def remote(source, target, send, recv, where):
        return pltpu.make_async_remote_copy(
            src_ref=source, dst_ref=target, send_sem=send, recv_sem=recv,
            device_id=where, device_id_type=pl.DeviceIdType.MESH,
        )

    columns = pl.ds(pl.multiple_of(core * block_len, block_len), block_len)

    def strip(i):
        return pl.ds(pl.multiple_of(i * wide, wide), wide)

    def load(i):
        rows = pl.ds(pl.multiple_of(core * mine + i * wide, wide), wide)
        return pltpu.make_async_copy(strain_ref.at[rows], data.at[strip(i), columns], load_sem.at[i])

    def swap(i):
        rows = pl.ds(pl.multiple_of((1 - core) * mine + i * wide, wide), wide)
        return remote(
            strain_ref.at[rows], data.at[strip(i), columns], swap_send.at[i], swap_recv.at[i], partner
        )

    def halo_copy(i, to):
        at = pl.multiple_of(i * wide + core * ROWS, ROWS)
        source = strain_ref.at[
            pl.ds(pl.multiple_of(to * mine + at, ROWS), ROWS),
            pl.ds(pl.multiple_of(core * half_len, half_len), half_len),
        ]
        return remote(
            source, halo.at[pl.ds(at, ROWS)], halo_send.at[to, i], halo_recv.at[core, i],
            device(chip - 1 + 2 * core, to),
        )

    def halo_arrival(i, side):
        block = halo.at[pl.ds(pl.multiple_of(i * wide + side * ROWS, ROWS), ROWS)]
        return remote(block, block, halo_send.at[0, i], halo_recv.at[side, i], partner)

    sends_halo = jnp.where(core == 0, has_left.astype(jnp.int32), has_right.astype(jnp.int32)) == 1

    @pl.loop(0, steps)
    def _(i):
        load(i).start()

    barrier = pltpu.get_barrier_semaphore()

    def greet(where):
        pl.semaphore_signal(barrier, inc=1, device_id=where, device_id_type=pl.DeviceIdType.MESH)

    greet(partner)
    for k in range(1, SPAN):
        greet(z_peer(k))
        greet(x_peer(k))
    for k in range(1, chan_count):
        greet({"chan": lax.rem(chan + k, chan_count)})
    for flag, shift, both in ((has_left, -1, 0), (has_right, 1, 1)):
        @pl.when(flag)
        def _():
            greet(device(chip + shift, 1 - both))

            @pl.when(core == both)
            def _():
                greet(device(chip + shift, both))
    left_count = has_left.astype(jnp.int32) * (2 - core)
    right_count = has_right.astype(jnp.int32) * (1 + core)
    pl.semaphore_wait(barrier, left_count + right_count + 1 + 2 * (SPAN - 1) + chan_count - 1)

    @pl.loop(0, steps)
    def _(i):
        swap(i).start()

        @pl.when(sends_halo)
        def _():
            for to in range(CORES):
                halo_copy(i, to).start()

    nyq_rows[...] = jnp.zeros_like(nyq_rows)
    consts = (window_ref, first_ref, second_ref, twist_ref)
    scratch = (buf, zbuf, ebuf, psum)

    def slab(i):
        return pl.ds(pl.multiple_of(i * ROWS, ROWS), ROWS)

    def way(i):
        return 1 - 2 * lax.rem(i, 2)

    def z_block(i, step):
        return sums.at[slab(i), lax.rem(z + step + SPAN, SPAN)]

    def x_block(i, step):
        return sums.at[slab(i), z, lax.rem(x + step + SPAN, SPAN)]

    def z_copy(kind, i):
        d = way(i)
        block, hop = ((2, d), (-d, -d), (d, d))[kind]
        return remote(z_block(i, block), z_in.at[kind, i], z_send.at[kind, i], z_recv.at[kind, i], z_peer(hop))

    def x_copy(kind, i):
        d = way(i)
        block, hop = ((2, d), (-d, -d), (d, d))[kind]
        return remote(x_block(i, block), x_in.at[kind, i], x_send.at[kind, i], x_recv.at[kind, i], x_peer(hop))

    def core_copy(i):
        rows = pl.ds(pl.multiple_of(i * ROWS * ROWS, ROWS * ROWS), ROWS * ROWS)
        return remote(fin.at[rows], from_partner.at[rows], core_send.at[i], core_recv.at[i], partner)

    def advance(copy, block, inbox, i):
        copy(0, i).wait_recv()
        target = block(i, way(i))
        target[...] = target[...] + inbox[0, i]
        copy(2, i).start()

    def collect(copy, block, inbox, i):
        copy(1, i).wait_recv()
        copy(2, i).wait_recv()
        return block(i, 0)[...] + inbox[1, i] + inbox[2, i]

    def nyq_copy(level, k):
        where = (z_peer, x_peer)[level](k)
        return remote(nyq_out.at[level], nyq_in.at[level, k], nyq_send.at[level, k], nyq_recv.at[level, k], where)

    def nyq_final():
        return remote(nyq_out.at[2], nyq_partner, nyq_core_send, nyq_core_recv, partner)

    @pl.loop(0, steps + 4)
    def _(t):
        @pl.when(t < steps)
        def _():
            load(t).wait()
            swap(t).wait_recv()
            for side in range(2):
                part = pl.ds(pl.multiple_of(t * wide + side * ROWS, ROWS), ROWS)

                def wait_halo():
                    @pl.when(exists[side])
                    def _():
                        halo_arrival(t, side).wait_recv()

                    @pl.when(jnp.logical_not(exists[side]))
                    def _():
                        halo[part, :] = jnp.zeros((ROWS, half_len), jnp.float32)

                nyq = side_sums(side, data.at[part], halo.at[part], on[side], wait_halo, consts, scratch)
                nyq_rows[part, :] = jnp.broadcast_to(nyq, (ROWS, ROOT))
            for r in range(ROWS):
                turned = jnp.transpose(psum[r * ROOT : (r + 1) * ROOT, :])
                sums[t * ROWS + r] = turned.reshape(sums.shape[1:])
            z_copy(0, t).start()
            z_copy(1, t).start()

        @pl.when(t == steps - 1)
        def _():
            turned = jnp.transpose(nyq_rows[...])
            nyq_out[0] = turned[:ROWS]
            for k in range(1, SPAN):
                nyq_copy(0, k).start()

        @pl.when(t >= 4)
        def _():
            i = t - 4
            fin[pl.ds(pl.multiple_of(i * ROWS * ROWS, ROWS * ROWS), ROWS * ROWS), :] = collect(
                x_copy, x_block, x_in, i
            ).reshape(ROWS * ROWS, ROOT)
            core_copy(i).start()

        @pl.when(jnp.logical_and(t >= 3, t < steps + 3))
        def _():
            advance(x_copy, x_block, x_in, t - 3)

        @pl.when(jnp.logical_and(t >= 2, t < steps + 2))
        def _():
            i = t - 2
            z_block(i, 0)[...] = collect(z_copy, z_block, z_in, i)
            x_copy(0, i).start()
            x_copy(1, i).start()

        @pl.when(jnp.logical_and(t >= 1, t < steps + 1))
        def _():
            advance(z_copy, z_block, z_in, t - 1)

        for level in range(2):
            @pl.when(t == steps + level)
            def _():
                total = nyq_out[level]
                for k in range(1, SPAN):
                    nyq_copy(level, k).wait_recv()
                    total = total + nyq_in[level, k]
                nyq_out[level + 1] = total
                if level == 0:
                    for k in range(1, SPAN):
                        nyq_copy(1, k).start()
                else:
                    nyq_final().start()

    nyq_final().wait_recv()
    for source in range(CORES):
        row = jnp.where(core == source, nyq_out[2], nyq_partner[...])
        nyquist_ref[source : source + 1, :] = row[:1] * scale

    lanes = lax.broadcasted_iota(jnp.int32, (1, ROOT), 1)
    column = [jnp.zeros((1, ROOT), jnp.float32) for _ in range(2)]
    for which, block in enumerate((fin, from_partner)):
        if which == 1:
            @pl.loop(0, steps)
            def _(i):
                core_copy(i).wait_recv()
        base = (core if which == 0 else 1 - core) * mine
        count = block.shape[0] // ROWS
        for j in range(2):
            both = jnp.concatenate(
                [
                    block[pl.ds(SPAN * core + j, count, stride=ROWS), :],
                    block[pl.ds(SPAN * core + 2 + j, count, stride=ROWS), :],
                ],
                axis=1,
            )
            placed = jnp.dot(
                both, mirror_ref[...], precision=lax.Precision.HIGHEST, preferred_element_type=jnp.float32
            )
            factor = jnp.where(jnp.logical_and(lanes == 0, me + j == 0), scale, 2.0 * scale)
            for side in range(2):
                value = placed[:, side * ROOT : (side + 1) * ROOT] * factor
                column[j] = column[j] + jnp.sum(value, axis=0, keepdims=True)
                for i in range(count // ROWS):
                    rows = pl.ds(pl.multiple_of(base + i * wide + side * ROWS, ROWS), ROWS)
                    power_ref[rows, j * ROOT : (j + 1) * ROOT] = value[i * ROWS : (i + 1) * ROWS]
    for j in range(2):
        channel_sums[j : j + 1, :] = column[j]

    def chan_copy(k):
        return remote(
            channel_sums, channel_from.at[k], chan_send.at[k], chan_recv.at[k],
            {"chan": lax.rem(chan + k, chan_count)},
        )

    for k in range(1, chan_count):
        chan_copy(k).start()

    @pl.loop(0, steps)
    def _(i):
        swap(i).wait_send()
        core_copy(i).wait_send()

        @pl.when(sends_halo)
        def _():
            for to in range(CORES):
                halo_copy(i, to).wait_send()

        for kind in range(3):
            z_copy(kind, i).wait_send()
            x_copy(kind, i).wait_send()

    for level in range(2):
        for k in range(1, SPAN):
            nyq_copy(level, k).wait_send()
    nyq_final().wait_send()

    channel_from[0] = channel_sums[...]
    for k in range(1, chan_count):
        chan_copy(k).wait()
    total = jnp.zeros_like(channel_sums)
    for source in range(chan_count):
        total = total + channel_from[lax.rem(chan - source + chan_count, chan_count)]
    mean_ref[...] = total * (1.0 / (CORES * mine * chan_count))


def per_device(strain):
    chan_rows, time_width = strain.shape
    seg_len = ROOT * ROOT
    half_len = seg_len // 2
    tm_count = lax.axis_size("tm")
    wide = 2 * ROWS
    mine = chan_rows // CORES
    assert time_width == seg_len and tm_count == SPAN * SPAN * CORES and mine % wide == 0 and mine <= ROOT
    segments = 2 * tm_count - 1
    band = half_len // tm_count
    first_all, second_all, twist, window, mirror, energy = tables(tm_count)
    pairs = mine // 2
    steps = mine // wide
    chan_count = lax.axis_size("chan")
    vmem = pl.BlockSpec(memory_space=pltpu.VMEM)
    f32 = jnp.float32
    dma = pltpu.SemaphoreType.DMA
    power, nyquist, mean_power = pl.pallas_call(
        functools.partial(welch_kernel, 1.0 / (segments * energy)),
        in_specs=[pl.BlockSpec(memory_space=pl.ANY)] + [vmem] * 5,
        out_specs=[vmem] * 3,
        out_shape=[
            jax.ShapeDtypeStruct((chan_rows, band), f32),
            jax.ShapeDtypeStruct((CORES, ROOT), f32),
            jax.ShapeDtypeStruct((2, ROOT), f32),
        ],
        scratch_shapes=[
            pltpu.VMEM((mine, CORES * seg_len), f32),
            pltpu.VMEM((mine, half_len), f32),
            pltpu.VMEM((pairs, SPAN, SPAN, ROWS, ROOT), f32),
            pltpu.VMEM((pairs * ROWS, ROOT), f32),
            pltpu.VMEM((pairs * ROWS, ROOT), f32),
            pltpu.VMEM((3, steps, ROWS, SPAN, ROWS, ROOT), f32),
            pltpu.VMEM((3, steps, ROWS, ROWS, ROOT), f32),
            pltpu.VMEM((ROOT, ROOT), f32),
            pltpu.VMEM((3, ROWS, ROOT), f32),
            pltpu.VMEM((2, SPAN, ROWS, ROOT), f32),
            pltpu.VMEM((ROWS, ROOT), f32),
            pltpu.VMEM((ROWS * ROOT, ROOT), f32),
            pltpu.VMEM((ROWS * 2 * CORES * HALF, 4 * ROOT), jnp.bfloat16),
            pltpu.VMEM((2 * CORES * ROWS, 6 * ROOT), jnp.bfloat16),
            pltpu.VMEM((ROWS * ROOT, ROOT), f32),
            pltpu.VMEM((2, ROOT), f32),
            pltpu.VMEM((chan_count, 2, ROOT), f32),
            dma((steps,)),
            dma((steps,)),
            dma((steps,)),
            dma((CORES, steps)),
            dma((2, steps)),
            dma((3, steps)),
            dma((3, steps)),
            dma((3, steps)),
            dma((3, steps)),
            dma((steps,)),
            dma((steps,)),
            dma((2, SPAN)),
            dma((2, SPAN)),
            dma(()),
            dma(()),
            dma((chan_count,)),
            dma((chan_count,)),
        ],
        compiler_params=pltpu.CompilerParams(
            collective_id=0, has_side_effects=True, vmem_limit_bytes=60 * 2**20
        ),
        name="welch",
    )(strain, window, first_all, second_all, twist, mirror)
    return (power, nyquist[:, :mine].reshape(-1), mean_power.reshape(-1))


def solution(mesh):
    in_specs = (P("chan", "tm"),)
    out_specs = (P("chan", "tm"), P("chan"), P("tm"))
    return jax.shard_map(
        per_device, mesh=mesh, in_specs=in_specs, out_specs=out_specs, check_vma=False
    )
```

time: 215 us -> 99 us (0.46)
  Pallas kernels: 210 us -> 93.8 us
    pallas_call x1, Pallas kernels: 210 us -> 93.8 us  [per_device(): pl.pallas_call(functools.partial(welch_kernel, 1.0 / (segments * energy))...]
where the time goes in v1:
time: 99 us; the launch traced here: 98.5 us
  Pallas kernels  93.8 us (95%)
  local copies, waits for them, and re-layouts  4.07 us (4%)
    pallas_call x1, Pallas kernels, per_device(): pl.pallas_call(functools.partial(welch_kernel, 1.0 / (segments * energy))...  93.8 us
    unnamed x2, local copies, waits for them, and re-layouts  2.81 us

profile of v1, /device:TPU:1, one launch (start us, length us, event | category | flops | bytes accessed | tf_op | source)
XLA Modules:
  0.0 98.5 jit_solution(16073290299317833326)
XLA Ops:
  0.6 93.8 %welch.1 = (f32[192,256]{1,0:T(8,128)}, f32[2,128]{1,0:T(2,128)}, f32[2,128]{1,0:T(2,128)}) custom-call(f32[192,16384]{1,0:T(8,128)} %strain_ref.1, f32[128,128]{1,0:T(8,128)} %constant.10.clone.window_ref, bf16[256,256]{1,0:T(8,128)(2,1)} %constant.11.clone.first_ref, bf16[768,256]{1,0:T(8,128)(2,1)} %constant.12.clone.second_ref, ...), custom_call_target="tpu_custom_call" | custom-call | tf_op jit(solution)/shard_map/welch/pallas_call | solution.py:478
  94.5 1.3 %reshape.12 = f32[192]{0:T(256)} reshape(f32[2,96]{1,0:T(2,128)} %bitcast.3) | data formatting | bytes 1536 | tf_op jit(solution)/shard_map/reshape | solution.py:528
  95.7 1.6 %copy.11 = f32[192,256]{1,0:T(8,128)} copy(f32[192,256]{1,0:T(8,128)} %get-tuple-element.12) | data formatting | bytes 393216
  97.3 1.2 %copy.12 = f32[256]{0:T(256)} copy(f32[256]{0:T(256)} %bitcast.2) | data formatting | bytes 2048

commit v2 on v1

v2 whole, which is shorter than its diff:
```python
import functools

import jax
import jax.numpy as jnp
import numpy as np
from jax import lax
from jax.experimental import pallas as pl
from jax.experimental.pallas import tpu as pltpu
from jax.sharding import PartitionSpec as P

ROOT = 128
HALF = ROOT // 2
ROWS = 8


def split_np(table):
    table = table.astype(np.float32)
    high = table.astype(jnp.bfloat16)
    low = (table - high.astype(np.float32)).astype(jnp.bfloat16)
    return high, low


@functools.cache
def tables(tm_count):
    pos = np.arange(ROOT)
    short = 2.0 * np.pi * (np.outer(pos, pos) % ROOT) / ROOT
    cos_s, sin_s = np.cos(short), np.sin(short)
    first = np.concatenate([cos_s[:HALF], -sin_s[:HALF]], axis=0)
    first_hi, first_lo = split_np(first)
    first_all = np.concatenate(
        [
            np.concatenate([first_hi, first_hi], axis=1),
            np.concatenate([first_lo, first_lo], axis=1),
        ],
        axis=0,
    )
    bands = np.arange(HALF).reshape(tm_count, HALF // tm_count)
    order = np.concatenate([bands, ROOT - 1 - bands], axis=1).reshape(-1)
    cos_o, sin_o = cos_s[:, order], sin_s[:, order]
    second = np.concatenate(
        [np.concatenate([cos_o, -sin_o], axis=1), np.concatenate([sin_o, cos_o], axis=1)], axis=0
    )
    second_hi, second_lo = split_np(second)
    second_all = np.concatenate([second_hi, second_hi, second_lo], axis=0)
    long = 2.0 * np.pi * np.outer(np.arange(HALF + ROWS), pos) / (ROOT * ROOT)
    twist = np.concatenate([np.cos(long), np.sin(long)], axis=1).astype(np.float32)
    mirror = np.zeros((2 * ROOT, 2 * ROOT), np.float32)
    for side in range(2):
        for k in range(HALF):
            mirror[side * HALF + k, side * ROOT + k] = 1.0
            mirror[ROOT + side * HALF + k, side * ROOT + (ROOT - k if k else HALF)] = 1.0
    seg_len = ROOT * ROOT
    window = 0.5 - 0.5 * np.cos(2.0 * np.pi * np.arange(seg_len) / seg_len)
    energy = float(np.sum(window * window))
    return first_all, second_all, twist, window.reshape(ROOT, ROOT).astype(np.float32), mirror, energy


def split(value):
    high = value.astype(jnp.bfloat16)
    low = (value - high.astype(jnp.float32)).astype(jnp.bfloat16)
    return high, low


SPAN = 4
CORES = 2


RELAYED = (2, 4, 5)
RELAY_AT = (2, 6, 8)


def half_sum(ref):
    parts = [ref[:, ROOT * a : ROOT * (a + 1)] for a in range(HALF)]
    while len(parts) > 1:
        parts = [parts[n] + parts[n + 1] for n in range(0, len(parts), 2)]
    return jnp.sum(parts[0], axis=1, keepdims=True)


def stage_one(piece, mean, consts, buf, zbuf, ebuf, seg, segs):
    window_ref, first_ref, _, twist_ref = consts
    mean = jnp.broadcast_to(mean, (ROWS, ROOT))
    even = jnp.zeros((ROWS, ROOT), jnp.float32)
    odd = jnp.zeros((ROWS, ROOT), jnp.float32)
    for a in range(ROOT):
        tile = (piece[:, ROOT * a : ROOT * (a + 1)] - mean) * window_ref[a : a + 1, :]
        buf[ROWS * a : ROWS * (a + 1), :] = tile
        if a % 2 == 0:
            even = even + tile
        else:
            odd = odd + tile
    alt = even - odd
    sign = (1 - 2 * (lax.broadcasted_iota(jnp.int32, (ROWS, ROOT), 1) % 2)).astype(jnp.float32)
    edge = jnp.sum((even + odd) * sign, axis=1, keepdims=True)
    turn = twist_ref[HALF : HALF + 1, :]
    high, low = split(jnp.concatenate([alt * turn[:, :ROOT], -alt * turn[:, ROOT:]], axis=1))
    ebuf[seg * ROWS : (seg + 1) * ROWS, :] = jnp.concatenate([high, low, high], axis=1)
    cos_t, sin_t = twist_ref[:HALF, :ROOT], twist_ref[:HALF, ROOT:]
    for r in range(0, ROWS, 2):
        pair = jnp.concatenate(
            [buf[pl.ds(r, ROOT, stride=ROWS), :], buf[pl.ds(r + 1, ROOT, stride=ROWS), :]], axis=1
        )
        high, low = split(pair)
        out = jnp.dot(
            first_ref[...], jnp.concatenate([high, low], axis=0), preferred_element_type=jnp.float32
        )
        out = out[:ROOT] + out[ROOT:]
        for s in range(2):
            re = out[:HALF, s * ROOT : (s + 1) * ROOT]
            im = out[HALF:, s * ROOT : (s + 1) * ROOT]
            z_hi, z_lo = split(
                jnp.concatenate([re * cos_t + im * sin_t, im * cos_t - re * sin_t], axis=1)
            )
            at = ((r + s) * segs + seg) * HALF
            zbuf[at : at + HALF, 0 : 2 * ROOT] = z_hi
            zbuf[at : at + HALF, 2 * ROOT :] = z_lo
    return edge * edge


def squares(left, right):
    out = jnp.dot(left, right, preferred_element_type=jnp.float32)
    return out[:, :ROOT] * out[:, :ROOT] + out[:, ROOT:] * out[:, ROOT:]


def group_sums(side, rows, on, wait_halo, consts, scratch):
    second_ref = consts[2]
    buf, zbuf, ebuf, psum = scratch
    half_len = ROOT * HALF
    segs = 2 * CORES
    lane = lax.broadcasted_iota(jnp.int32, (ROWS, ROOT), 1)

    def window(start, length):
        return rows.at[:, pl.ds(pl.multiple_of(start, half_len), length)]

    own = side * half_len
    totals = [half_sum(window(own + h * half_len, half_len)) for h in range(segs)]
    inverse = 1.0 / (2 * half_len)
    nyq = jnp.zeros((ROWS, 1), jnp.float32)
    for seg in range(segs - 1):
        nyq = nyq + stage_one(
            window(own + seg * half_len, 2 * half_len), (totals[seg] + totals[seg + 1]) * inverse,
            consts, buf, zbuf, ebuf, seg, segs,
        )
    wait_halo()
    near = jnp.where(side == 0, totals[-1], totals[0])
    far = half_sum(window((1 - side) * segs * half_len, half_len))
    nyq = nyq + on * stage_one(
        window((1 - side) * (segs - 1) * half_len, 2 * half_len), (near + far) * inverse,
        consts, buf, zbuf, ebuf, segs - 1, segs,
    )

    def fold(power, count):
        total = power[:count]
        for seg in range(1, segs - 1):
            total = total + power[seg * count : (seg + 1) * count]
        return total + on * power[(segs - 1) * count :]

    for r in range(ROWS):
        at = slice(r * segs * HALF, (r + 1) * segs * HALF)
        left = jnp.concatenate([zbuf[at, :], zbuf[at, : 2 * ROOT]], axis=1)
        psum[r * HALF : (r + 1) * HALF, :] = fold(squares(left, second_ref[...]), HALF)
    mixed = fold(squares(ebuf[...], second_ref[...]), ROWS)
    first_rows = pl.ds(0, ROWS, stride=HALF)
    psum[first_rows, :] = jnp.where(lane % SPAN >= SPAN // 2, mixed, psum[first_rows, :])
    return nyq


def welch_kernel(
    scale, strain_ref, window_ref, first_ref, second_ref, twist_ref, mirror_ref,
    power_ref, nyquist_ref, mean_ref,
    data, relay_box, sums, fin, from_partner, z_in, x_in, nyq_rows, nyq_out, nyq_in, nyq_partner,
    buf, zbuf, ebuf, psum, mean_out, mean_in,
    load_sem, swap_send, swap_recv, halo_send, halo_recv, relay_send, relay_recv,
    z_send, z_recv, x_send, x_recv, core_send, core_recv,
    nyq_send, nyq_recv, nyq_core_send, nyq_core_recv, mean_send, mean_recv,
):
    chan, chan_count = lax.axis_index("chan"), lax.axis_size("chan")
    me = lax.axis_index("tm")
    core = lax.rem(me, CORES)
    chip = me // CORES
    chips = lax.axis_size("tm") // CORES
    z, x = chip // SPAN, lax.rem(chip, SPAN)
    half_len = ROOT * HALF
    block_len = 2 * half_len
    mine = data.shape[0]
    groups = mine // ROWS
    tile = ROWS // 2
    batches = groups // 2
    has_left, has_right = chip > 0, chip < chips - 1
    exists = (has_right, has_left)

    def as_int(flag):
        return flag.astype(jnp.int32)

    def device(chip_index, core_index):
        return {"tm": chip_index * CORES + core_index}

    def z_peer(step):
        return device(lax.rem(z + step + SPAN, SPAN) * SPAN + x, core)

    def x_peer(step):
        return device(z * SPAN + lax.rem(x + step + SPAN, SPAN), core)

    partner = device(chip, 1 - core)
    toward = 2 * core - 1
    sends_halo = jnp.where(core == 0, as_int(has_left), as_int(has_right)) == 1
    at_column = jnp.logical_or(x == 0, x == SPAN - 1)
    has_next_row = jnp.where(core == 0, as_int(z > 0), as_int(z < SPAN - 1)) == 1
    linked = jnp.logical_and(at_column, has_next_row)
    crosses = jnp.logical_and(linked, x == (SPAN - 1) * core)
    relays = jnp.logical_and(linked, x == (SPAN - 1) * (1 - core))
    faces = x == (SPAN - 1) * (1 - core)
    next_row = device(chip + toward * SPAN, 1 - core)

    def across(core_index):
        return device(z * SPAN + (SPAN - 1) - x, core_index)

    def remote(source, target, send, recv, where):
        return pltpu.make_async_remote_copy(
            src_ref=source, dst_ref=target, send_sem=send, recv_sem=recv,
            device_id=where, device_id_type=pl.DeviceIdType.MESH,
        )

    def strip(g):
        return pl.ds(pl.multiple_of(g * ROWS, ROWS), ROWS)

    def columns(g):
        start = lax.rem(g, 2) * half_len + core * block_len
        return pl.ds(pl.multiple_of(start, half_len), block_len)

    def load(g):
        rows = pl.ds(pl.multiple_of(core * mine + g * ROWS, ROWS), ROWS)
        return pltpu.make_async_copy(strain_ref.at[rows], data.at[strip(g), columns(g)], load_sem.at[g])

    def swap(g):
        rows = pl.ds(pl.multiple_of((1 - core) * mine + g * ROWS, ROWS), ROWS)
        return remote(
            strain_ref.at[rows], data.at[strip(g), columns(g)], swap_send.at[g], swap_recv.at[g], partner
        )

    def halo_place(n, side):
        start = (1 - side) * 2 * CORES * half_len
        return data.at[strip(2 * n + side), pl.ds(pl.multiple_of(start, half_len), half_len)]

    def halo_source(n, to):
        return strain_ref.at[
            pl.ds(pl.multiple_of(to * mine + (2 * n + core) * ROWS, ROWS), ROWS),
            pl.ds(pl.multiple_of(core * half_len, half_len), half_len),
        ]

    def halo_copy(n, to):
        return remote(
            halo_source(n, to), halo_place(n, core), halo_send.at[to, n], halo_recv.at[core, n],
            device(chip + toward, to),
        )

    def relay_copy(k, to):
        n = RELAYED[k]
        return remote(
            halo_source(n, to), relay_box.at[k, to], halo_send.at[to, n], relay_recv.at[k, to], next_row
        )

    def relay_on(k, to):
        n = RELAYED[k]
        return remote(
            relay_box.at[k, to], halo_place(n, 1 - core), relay_send.at[k, to],
            halo_recv.at[1 - core, n], across(to),
        )

    def halo_arrival(n, side):
        block = halo_place(n, side)
        return remote(block, block, halo_send.at[0, n], halo_recv.at[side, n], partner)

    @pl.loop(0, groups)
    def _(g):
        load(g).start()

    barrier = pltpu.get_barrier_semaphore()

    def greet(where):
        pl.semaphore_signal(barrier, inc=1, device_id=where, device_id_type=pl.DeviceIdType.MESH)

    def mean_peer(other, k):
        where = {"chan": lax.rem(chan + k, chan_count)}
        if other:
            where["tm"] = chip * CORES + 1 - core
        return where

    greet(partner)
    for k in range(1, SPAN):
        greet(z_peer(k))
        greet(x_peer(k))
    for k in range(1, chan_count):
        for other in range(2):
            greet(mean_peer(other, k))
    for flag, shift, both in ((has_left, -1, 0), (has_right, 1, 1)):
        @pl.when(flag)
        def _():
            greet(device(chip + shift, 1 - both))

            @pl.when(core == both)
            def _():
                greet(device(chip + shift, both))

    @pl.when(linked)
    def _():
        greet(next_row)

    @pl.when(faces)
    def _():
        greet(across(1 - core))

    left_count = as_int(has_left) * (2 - core)
    right_count = as_int(has_right) * (1 + core)
    pl.semaphore_wait(
        barrier,
        left_count + right_count + as_int(linked) + as_int(faces) + 1 + 2 * (SPAN - 1) + 2 * (chan_count - 1),
    )

    for n in range(batches):
        for side in range(2):
            swap(2 * n + side).start()

        @pl.when(sends_halo)
        def _():
            for to in range(CORES):
                if n in RELAYED:
                    @pl.when(crosses)
                    def _():
                        relay_copy(RELAYED.index(n), to).start()

                    @pl.when(jnp.logical_not(crosses))
                    def _():
                        halo_copy(n, to).start()
                else:
                    halo_copy(n, to).start()

    nyq_rows[...] = jnp.zeros_like(nyq_rows)
    consts = (window_ref, first_ref, second_ref, twist_ref)
    scratch = (buf, zbuf, ebuf, psum)

    def slab(i, size):
        return pl.ds(pl.multiple_of(i * size, size), size)

    def way(i):
        return 1 - 2 * lax.rem(i, 2)

    def z_block(i, step):
        return sums.at[slab(i, tile), lax.rem(z + step + SPAN, SPAN)]

    def x_block(i, step):
        return sums.at[slab(i, ROWS), z, lax.rem(x + step + SPAN, SPAN)]

    def ring(kind, i, block, inbox, send, recv, peer):
        d = way(i)
        step, hop = ((2, d), (-d, -d), (d, d))[kind]
        return remote(block(i, step), inbox.at[kind, i], send.at[kind, i], recv.at[kind, i], peer(hop))

    def z_copy(kind, i):
        return ring(kind, i, z_block, z_in, z_send, z_recv, z_peer)

    def x_copy(kind, i):
        return ring(kind, i, x_block, x_in, x_send, x_recv, x_peer)

    def core_copy(i):
        rows = slab(i, ROWS * ROWS)
        return remote(fin.at[rows], from_partner.at[rows], core_send.at[i], core_recv.at[i], partner)

    def begin(copy, i):
        copy(0, i).start()
        copy(1, i).start()

    def advance(copy, block, inbox, i):
        copy(0, i).wait_recv()
        target = block(i, way(i))
        target[...] = target[...] + inbox[0, i]
        copy(2, i).start()

    def collect(copy, block, inbox, i):
        copy(1, i).wait_recv()
        copy(2, i).wait_recv()
        return block(i, 0)[...] + inbox[1, i] + inbox[2, i]

    def z_advance(i):
        advance(z_copy, z_block, z_in, i)

    def z_collect(i):
        z_block(i, 0)[...] = collect(z_copy, z_block, z_in, i)

    def x_advance(i):
        advance(x_copy, x_block, x_in, i)

    def x_collect(i):
        fin[slab(i, ROWS * ROWS), :] = collect(x_copy, x_block, x_in, i).reshape(ROWS * ROWS, ROOT)
        core_copy(i).start()

    def nyq_copy(level, k):
        where = (z_peer, x_peer)[level](k)
        return remote(nyq_out.at[level], nyq_in.at[level, k], nyq_send.at[level, k], nyq_recv.at[level, k], where)

    def nyq_begin(level):
        nyq_in[level, 0] = nyq_out[level]
        for k in range(1, SPAN):
            nyq_copy(level, k).start()

    def nyq_collect(level):
        for k in range(1, SPAN):
            nyq_copy(level, k).wait_recv()
        here = (z, x)[level]
        total = nyq_in[level, lax.rem(here + SPAN, SPAN)]
        for source in range(1, SPAN):
            total = total + nyq_in[level, lax.rem(here - source + SPAN, SPAN)]
        nyq_out[level + 1] = total

    def nyq_final():
        return remote(nyq_out.at[2], nyq_partner, nyq_core_send, nyq_core_recv, partner)

    @pl.loop(0, groups)
    def _(t):
        side = lax.rem(t, 2)
        here = jnp.where(side == 0, as_int(has_right), as_int(has_left))
        load(t).wait()
        swap(t).wait_recv()

        for k in range(len(RELAYED)):
            @pl.when(jnp.logical_and(relays, t == RELAY_AT[k]))
            def _():
                for to in range(CORES):
                    relay_copy(k, to).wait_recv()
                    relay_on(k, to).start()

        def wait_halo():
            @pl.when(here == 1)
            def _():
                halo_arrival(t // 2, side).wait_recv()

            @pl.when(here == 0)
            def _():
                place = halo_place(t // 2, side)
                place[...] = jnp.zeros((ROWS, half_len), jnp.float32)

        nyq = group_sums(side, data.at[strip(t)], here.astype(jnp.float32), wait_halo, consts, scratch)
        nyq_rows[strip(t), :] = jnp.broadcast_to(nyq, (ROWS, ROOT))
        for p in range(tile):
            turned = jnp.transpose(psum[p * ROOT : (p + 1) * ROOT, :])
            sums[t * tile + p] = turned.reshape(sums.shape[1:])
        begin(z_copy, t)

        @pl.when(t >= 2)
        def _():
            z_advance(t - 2)

        @pl.when(t >= 4)
        def _():
            z_collect(t - 4)

    turned = jnp.transpose(nyq_rows[...])
    nyq_out[0] = turned[:ROWS]
    nyq_begin(0)
    early = batches - 2
    for b in range(early):
        begin(x_copy, b)
    z_advance(groups - 2)
    z_collect(groups - 4)
    z_collect(groups - 3)
    begin(x_copy, early)
    for b in range(early):
        x_advance(b)
    z_advance(groups - 1)
    nyq_collect(0)
    nyq_begin(1)
    x_advance(early)
    for b in range(early):
        x_collect(b)
    z_collect(groups - 2)
    z_collect(groups - 1)
    begin(x_copy, early + 1)
    nyq_collect(1)
    nyq_final().start()
    x_collect(early)
    x_advance(early + 1)
    x_collect(early + 1)

    lines = [fin[slab(i, ROWS), :] for i in range(fin.shape[0] // ROWS)]
    while len(lines) > 1:
        lines = [a + b for a, b in zip(lines[::2], lines[1::2])] + lines[len(lines) // 2 * 2 :]
    mean_out[...] = lines[0]

    def mean_copy(other, k):
        return remote(
            mean_out, mean_in.at[other, k], mean_send.at[other, k], mean_recv.at[other, k], mean_peer(other, k)
        )

    mean_links = [(other, k) for other in range(2) for k in range(chan_count) if other + k > 0]
    for link in mean_links:
        mean_copy(*link).start()
    mean_in[0, 0] = mean_out[...]

    nyq_final().wait_recv()
    for source in range(CORES):
        row = jnp.where(core == source, nyq_out[2], nyq_partner[...])
        nyquist_ref[source : source + 1, :] = row[:1] * scale

    lanes = lax.broadcasted_iota(jnp.int32, (1, ROOT), 1)

    def unfold(both):
        return jnp.dot(
            both, mirror_ref[...], precision=lax.Precision.HIGHEST, preferred_element_type=jnp.float32
        )

    factors = [jnp.where(jnp.logical_and(lanes == 0, me + j == 0), scale, 2.0 * scale) for j in range(2)]
    pairs = mine // 2
    for which, block in enumerate((fin, from_partner)):
        if which == 1:
            for b in range(batches):
                core_copy(b).wait_recv()
        base = (core if which == 0 else 1 - core) * mine
        for j in range(2):
            both = jnp.concatenate(
                [block[pl.ds(SPAN * core + j + shift, pairs, stride=ROWS), :] for shift in (0, 2)], axis=1
            )
            placed = unfold(both)
            for half in range(2):
                power_ref[pl.ds(j * CORES * mine + base + half, pairs, stride=2), :] = (
                    placed[:, half * ROOT : (half + 1) * ROOT] * factors[j]
                )

    for n in range(batches):
        for side in range(2):
            swap(2 * n + side).wait_send()
        core_copy(n).wait_send()

        @pl.when(sends_halo)
        def _():
            for to in range(CORES):
                halo_copy(n, to).wait_send()

        for kind in range(3):
            x_copy(kind, n).wait_send()

    @pl.loop(0, groups)
    def _(g):
        for kind in range(3):
            z_copy(kind, g).wait_send()

    @pl.when(relays)
    def _():
        for k in range(len(RELAYED)):
            for to in range(CORES):
                relay_on(k, to).wait_send()

    for level in range(2):
        for k in range(1, SPAN):
            nyq_copy(level, k).wait_send()
    nyq_final().wait_send()

    for link in mean_links:
        mean_copy(*link).wait()
    total = jnp.zeros((ROWS, ROOT), jnp.float32)
    for source_chan in range(chan_count):
        for source_core in range(CORES):
            total = total + mean_in[
                lax.rem(core + source_core, CORES), lax.rem(chan - source_chan + chan_count, chan_count)
            ]
    mean_out[...] = total
    rows = [mean_out[pl.ds(SPAN * core + j, 1), :] for j in range(SPAN)]
    placed = unfold(
        jnp.concatenate(
            [jnp.concatenate([rows[j], rows[j + 2]], axis=1) for j in range(2)]
            + [jnp.zeros((ROWS - 2, 2 * ROOT), jnp.float32)],
            axis=0,
        )
    )
    placed = placed[:, :ROOT] + placed[:, ROOT:]
    for j in range(2):
        mean_ref[j : j + 1, :] = placed[j : j + 1] * (factors[j] * (1.0 / (CORES * mine * chan_count)))


def per_device(strain):
    chan_rows, time_width = strain.shape
    seg_len = ROOT * ROOT
    half_len = seg_len // 2
    tm_count = lax.axis_size("tm")
    mine = chan_rows // CORES
    assert time_width == seg_len and tm_count == SPAN * SPAN * CORES and mine == 12 * ROWS
    segments = 2 * tm_count - 1
    first_all, second_all, twist, window, mirror, energy = tables(tm_count)
    pairs = mine // 2
    groups = mine // ROWS
    batches = groups // 2
    tile = ROWS // 2
    chan_count = lax.axis_size("chan")
    vmem = pl.BlockSpec(memory_space=pltpu.VMEM)
    f32 = jnp.float32
    dma = pltpu.SemaphoreType.DMA
    relayed = len(RELAYED)
    power, nyquist, mean_power = pl.pallas_call(
        functools.partial(welch_kernel, 1.0 / (segments * energy)),
        in_specs=[pl.BlockSpec(memory_space=pl.ANY)] + [vmem] * 5,
        out_specs=[vmem] * 3,
        out_shape=[
            jax.ShapeDtypeStruct((2 * chan_rows, ROOT), f32),
            jax.ShapeDtypeStruct((CORES, ROOT), f32),
            jax.ShapeDtypeStruct((2, ROOT), f32),
        ],
        scratch_shapes=[
            pltpu.VMEM((mine, CORES * seg_len + half_len), f32),
            pltpu.VMEM((relayed, CORES, ROWS, half_len), f32),
            pltpu.VMEM((pairs, SPAN, SPAN, ROWS, ROOT), f32),
            pltpu.VMEM((pairs * ROWS, ROOT), f32),
            pltpu.VMEM((pairs * ROWS, ROOT), f32),
            pltpu.VMEM((3, groups, tile, SPAN, ROWS, ROOT), f32),
            pltpu.VMEM((3, batches, ROWS, ROWS, ROOT), f32),
            pltpu.VMEM((ROOT, ROOT), f32),
            pltpu.VMEM((3, ROWS, ROOT), f32),
            pltpu.VMEM((2, SPAN, ROWS, ROOT), f32),
            pltpu.VMEM((ROWS, ROOT), f32),
            pltpu.VMEM((ROWS * ROOT, ROOT), f32),
            pltpu.VMEM((ROWS * 2 * CORES * HALF, 4 * ROOT), jnp.bfloat16),
            pltpu.VMEM((2 * CORES * ROWS, 6 * ROOT), jnp.bfloat16),
            pltpu.VMEM((ROWS * HALF, ROOT), f32),
            pltpu.VMEM((ROWS, ROOT), f32),
            pltpu.VMEM((2, chan_count, ROWS, ROOT), f32),
            dma((groups,)),
            dma((groups,)),
            dma((groups,)),
            dma((CORES, batches)),
            dma((2, batches)),
            dma((relayed, CORES)),
            dma((relayed, CORES)),
            dma((3, groups)),
            dma((3, groups)),
            dma((3, batches)),
            dma((3, batches)),
            dma((batches,)),
            dma((batches,)),
            dma((2, SPAN)),
            dma((2, SPAN)),
            dma(()),
            dma(()),
            dma((2, chan_count)),
            dma((2, chan_count)),
        ],
        compiler_params=pltpu.CompilerParams(
            collective_id=0, has_side_effects=True, vmem_limit_bytes=60 * 2**20
        ),
        name="welch",
    )(strain, window, first_all, second_all, twist, mirror)
    power = jnp.concatenate([power[:chan_rows], power[chan_rows:]], axis=1)
    return (power, nyquist[:, :mine].reshape(-1), mean_power.reshape(-1))


def solution(mesh):
    in_specs = (P("chan", "tm"),)
    out_specs = (P("chan", "tm"), P("chan"), P("tm"))
    return jax.shard_map(
        per_device, mesh=mesh, in_specs=in_specs, out_specs=out_specs, check_vma=False
    )
```

time: 99 us -> 81.1 us (0.82)
  Pallas kernels: 93.8 us -> 75.9 us
    pallas_call x1, Pallas kernels: 93.8 us -> 75.9 us  [per_device(): pl.pallas_call(functools.partial(welch_kernel, 1.0 / (segments * energy))...]
    unnamed x2 -> x1, local copies, waits for them, and re-layouts: 2.81 us -> 1.2 us
where the time goes in v2:
time: 81.1 us; the launch traced here: 80.7 us
  Pallas kernels  75.9 us (94%)
  local copies, waits for them, and re-layouts  3.43 us (4%)
    pallas_call x1, Pallas kernels, per_device(): pl.pallas_call(functools.partial(welch_kernel, 1.0 / (segments * energy))...  75.9 us

profile of v2, /device:TPU:1, one launch (start us, length us, event | category | flops | bytes accessed | tf_op | source)
XLA Modules:
  0.0 80.7 jit_solution(13339474461865394633)
XLA Ops:
  0.6 75.9 %welch.1 = (f32[384,128]{1,0:T(8,128)}, f32[2,128]{1,0:T(2,128)}, f32[2,128]{1,0:T(2,128)}) custom-call(f32[192,16384]{1,0:T(8,128)} %strain_ref.1, f32[128,128]{1,0:T(8,128)} %constant.10.clone.window_ref, bf16[256,256]{1,0:T(8,128)(2,1)} %constant.11.clone.first_ref, bf16[768,256]{1,0:T(8,128)(2,1)} %constant.12.clone.second_ref, ...), custom_call_target="tpu_custom_call" | custom-call | tf_op jit(solution)/shard_map/welch/pallas_call | solution.py:596
  76.6 1.3 %reshape.12 = f32[192]{0:T(256)} reshape(f32[2,96]{1,0:T(2,128)} %bitcast.3) | data formatting | bytes 1536 | tf_op jit(solution)/shard_map/reshape | solution.py:649
  77.8 1.0 %fusion = (f32[192,128]{1,0:T(8,128)S(1)}, f32[192,128]{1,0:T(8,128)S(1)}) fusion(f32[384,128]{1,0:T(8,128)} %get-tuple-element.6), kind=kLoop, calls=%fused_computation.1 | loop fusion | bytes 393216 | tf_op jit(solution)/shard_map/slice | solution.py:648
  78.8 0.7 pad_maximum_fusion
  79.5 1.2 %copy.10 = f32[256]{0:T(256)} copy(f32[256]{0:T(256)} %bitcast.2) | data formatting | bytes 2048

commit v3 on v2

--- a/solution.py
+++ b/solution.py
@@ -52,7 +52,7 @@
     seg_len = ROOT * ROOT
     window = 0.5 - 0.5 * np.cos(2.0 * np.pi * np.arange(seg_len) / seg_len)
     energy = float(np.sum(window * window))
-    return first_all, second_all, twist, window.reshape(ROOT, ROOT).astype(np.float32), mirror, energy
+    return first_all, second_all, twist, window.reshape(ROOT, ROOT).astype(np.float32), mirror.astype(jnp.bfloat16), energy
 
 
 def split(value):
@@ -66,7 +66,10 @@
 
 
 RELAYED = (2, 4, 5)
-RELAY_AT = (2, 6, 8)
+RELAY_AT = (2, 5, 7)
+HELD = 3
+RING_AT = (3, 7)
+X_START = ((9, 0, 4), (10, 4, 6), (11, 6, 8))
 
 
 def half_sum(ref):
@@ -165,13 +168,12 @@
 
 
 def welch_kernel(
-    scale, strain_ref, window_ref, first_ref, second_ref, twist_ref, mirror_ref,
-    power_ref, nyquist_ref, mean_ref,
-    data, relay_box, sums, fin, from_partner, z_in, x_in, nyq_rows, nyq_out, nyq_in, nyq_partner,
+    scale, strain_ref, window_hbm, first_hbm, second_hbm, twist_hbm, mirror_hbm, packed_ref,
+    window_ref, first_ref, second_ref, twist_ref, mirror_ref, power_box, small_box, table_sem, out_sem,
+    data, relay_box, sums, fin, from_partner, z_in, x_in, direct_in, nyq_box, nyq_rows,
     buf, zbuf, ebuf, psum, mean_out, mean_in,
     load_sem, swap_send, swap_recv, halo_send, halo_recv, relay_send, relay_recv,
-    z_send, z_recv, x_send, x_recv, core_send, core_recv,
-    nyq_send, nyq_recv, nyq_core_send, nyq_core_recv, mean_send, mean_recv,
+    z_send, z_recv, x_send, x_recv, direct_send, direct_recv, core_send, core_recv, mean_send, mean_recv,
 ):
     chan, chan_count = lax.axis_index("chan"), lax.axis_size("chan")
     me = lax.axis_index("tm")
@@ -185,6 +187,9 @@
     groups = mine // ROWS
     tile = ROWS // 2
     batches = groups // 2
+    ringed = groups
+    size = tile * ROWS
+    ring_at = jnp.where(jnp.logical_or(x == 0, x == SPAN - 1), RING_AT[1], RING_AT[0])
     has_left, has_right = chip > 0, chip < chips - 1
     exists = (has_right, has_left)
 
@@ -223,56 +228,55 @@
     def strip(g):
         return pl.ds(pl.multiple_of(g * ROWS, ROWS), ROWS)
 
-    def columns(g):
-        start = lax.rem(g, 2) * half_len + core * block_len
+    def columns(g, side):
+        start = side * half_len + core * block_len
         return pl.ds(pl.multiple_of(start, half_len), block_len)
 
     def load(g):
         rows = pl.ds(pl.multiple_of(core * mine + g * ROWS, ROWS), ROWS)
-        return pltpu.make_async_copy(strain_ref.at[rows], data.at[strip(g), columns(g)], load_sem.at[g])
+        place = data.at[strip(g), columns(g, lax.rem(g + core, 2))]
+        return pltpu.make_async_copy(strain_ref.at[rows], place, load_sem.at[g])
 
     def swap(g):
         rows = pl.ds(pl.multiple_of((1 - core) * mine + g * ROWS, ROWS), ROWS)
-        return remote(
-            strain_ref.at[rows], data.at[strip(g), columns(g)], swap_send.at[g], swap_recv.at[g], partner
-        )
-
-    def halo_place(n, side):
+        place = data.at[strip(g), columns(g, lax.rem(g + 1 - core, 2))]
+        return remote(strain_ref.at[rows], place, swap_send, swap_recv.at[g], partner)
+
+    def halo_group(n, side, to):
+        return 2 * n + lax.rem(side + to, 2)
+
+    def halo_place(n, side, to):
         start = (1 - side) * 2 * CORES * half_len
-        return data.at[strip(2 * n + side), pl.ds(pl.multiple_of(start, half_len), half_len)]
+        return data.at[strip(halo_group(n, side, to)), pl.ds(pl.multiple_of(start, half_len), half_len)]
 
     def halo_source(n, to):
         return strain_ref.at[
-            pl.ds(pl.multiple_of(to * mine + (2 * n + core) * ROWS, ROWS), ROWS),
+            pl.ds(pl.multiple_of(to * mine + halo_group(n, core, to) * ROWS, ROWS), ROWS),
             pl.ds(pl.multiple_of(core * half_len, half_len), half_len),
         ]
 
     def halo_copy(n, to):
         return remote(
-            halo_source(n, to), halo_place(n, core), halo_send.at[to, n], halo_recv.at[core, n],
+            halo_source(n, to), halo_place(n, core, to), halo_send, halo_recv.at[core, n],
             device(chip + toward, to),
         )
 
     def relay_copy(k, to):
         n = RELAYED[k]
         return remote(
-            halo_source(n, to), relay_box.at[k, to], halo_send.at[to, n], relay_recv.at[k, to], next_row
+            halo_source(n, to), relay_box.at[k, to], halo_send, relay_recv.at[k, to], next_row
         )
 
     def relay_on(k, to):
         n = RELAYED[k]
         return remote(
-            relay_box.at[k, to], halo_place(n, 1 - core), relay_send.at[k, to],
+            relay_box.at[k, to], halo_place(n, 1 - core, to), relay_send,
             halo_recv.at[1 - core, n], across(to),
         )
 
     def halo_arrival(n, side):
-        block = halo_place(n, side)
-        return remote(block, block, halo_send.at[0, n], halo_recv.at[side, n], partner)
-
-    @pl.loop(0, groups)
-    def _(g):
-        load(g).start()
+        block = halo_place(n, side, core)
+        return remote(block, block, halo_send, halo_recv.at[side, n], partner)
 
     barrier = pltpu.get_barrier_semaphore()
 
@@ -285,10 +289,13 @@
             where["tm"] = chip * CORES + 1 - core
         return where
 
+    def chip_peer(k):
+        far_z, far_x = lax.rem(z + k // SPAN, SPAN), lax.rem(x + k % SPAN, SPAN)
+        return far_z, far_x, device(far_z * SPAN + far_x, core)
+
     greet(partner)
-    for k in range(1, SPAN):
-        greet(z_peer(k))
-        greet(x_peer(k))
+    for k in range(1, SPAN * SPAN):
+        greet(chip_peer(k)[2])
     for k in range(1, chan_count):
         for other in range(2):
             greet(mean_peer(other, k))
@@ -309,11 +316,28 @@
     def _():
         greet(across(1 - core))
 
+    tables_in = [
+        pltpu.make_async_copy(source, target, table_sem.at[n])
+        for n, (source, target) in enumerate(
+            zip(
+                (window_hbm, first_hbm, second_hbm, twist_hbm, mirror_hbm),
+                (window_ref, first_ref, second_ref, twist_ref, mirror_ref),
+            )
+        )
+    ]
+    load(0).start()
+    for table in tables_in:
+        table.start()
+
+    @pl.loop(1, groups)
+    def _(g):
+        load(g).start()
+
     left_count = as_int(has_left) * (2 - core)
     right_count = as_int(has_right) * (1 + core)
     pl.semaphore_wait(
         barrier,
-        left_count + right_count + as_int(linked) + as_int(faces) + 1 + 2 * (SPAN - 1) + 2 * (chan_count - 1),
+        left_count + right_count + as_int(linked) + as_int(faces) + SPAN * SPAN + 2 * (chan_count - 1),
     )
 
     for n in range(batches):
@@ -322,12 +346,17 @@
 
         @pl.when(sends_halo)
         def _():
-            for to in range(CORES):
+            for turn in range(CORES):
+                to = lax.rem(core + turn, CORES)
                 if n in RELAYED:
                     @pl.when(crosses)
                     def _():
                         relay_copy(RELAYED.index(n), to).start()
 
+                    @pl.when(jnp.logical_not(crosses))
+                    def _():
+                        halo_copy(n, to).start()
+                elif n == HELD:
                     @pl.when(jnp.logical_not(crosses))
                     def _():
                         halo_copy(n, to).start()
@@ -335,6 +364,8 @@
                     halo_copy(n, to).start()
 
     nyq_rows[...] = jnp.zeros_like(nyq_rows)
+    for table in tables_in:
+        table.wait()
     consts = (window_ref, first_ref, second_ref, twist_ref)
     scratch = (buf, zbuf, ebuf, psum)
 
@@ -348,12 +379,12 @@
         return sums.at[slab(i, tile), lax.rem(z + step + SPAN, SPAN)]
 
     def x_block(i, step):
-        return sums.at[slab(i, ROWS), z, lax.rem(x + step + SPAN, SPAN)]
+        return sums.at[slab(i, tile), z, lax.rem(x + step + SPAN, SPAN)]
 
     def ring(kind, i, block, inbox, send, recv, peer):
         d = way(i)
         step, hop = ((2, d), (-d, -d), (d, d))[kind]
-        return remote(block(i, step), inbox.at[kind, i], send.at[kind, i], recv.at[kind, i], peer(hop))
+        return remote(block(i, step), inbox.at[kind, i], send, recv.at[kind, i], peer(hop))
 
     def z_copy(kind, i):
         return ring(kind, i, z_block, z_in, z_send, z_recv, z_peer)
@@ -362,8 +393,30 @@
         return ring(kind, i, x_block, x_in, x_send, x_recv, x_peer)
 
     def core_copy(i):
-        rows = slab(i, ROWS * ROWS)
-        return remote(fin.at[rows], from_partner.at[rows], core_send.at[i], core_recv.at[i], partner)
+        count = 2 * size + (ROWS if i == batches - 1 else 0)
+        rows = pl.ds(i * 2 * size, count)
+        return remote(fin.at[rows], from_partner.at[rows], core_send, core_recv.at[i], partner)
+
+    def direct_copy(k):
+        far_z, far_x, where = chip_peer(k)
+        return remote(nyq_box, direct_in.at[k], direct_send, direct_recv, where)
+
+    def direct_all():
+        box = direct_in.at[pl.ds(1, SPAN * SPAN - 1)]
+        return remote(box, box, direct_send, direct_recv, partner)
+
+    def send_direct():
+        for k in (10, 6, 9, 11, 14, 2, 8, 5, 7, 13, 15, 1, 3, 4, 12):
+            direct_copy(k).start()
+
+    def sum_direct():
+        direct_all().wait_recv()
+        nyq = jnp.zeros((ROWS, ROOT), jnp.float32)
+        for far_z in range(SPAN):
+            for far_x in range(SPAN):
+                k = lax.rem(z - far_z + SPAN, SPAN) * SPAN + lax.rem(x - far_x + SPAN, SPAN)
+                nyq = nyq + direct_in[k]
+        fin[pl.ds(groups * size, ROWS), :] = nyq
 
     def begin(copy, i):
         copy(0, i).start()
@@ -390,33 +443,12 @@
         advance(x_copy, x_block, x_in, i)
 
     def x_collect(i):
-        fin[slab(i, ROWS * ROWS), :] = collect(x_copy, x_block, x_in, i).reshape(ROWS * ROWS, ROOT)
-        core_copy(i).start()
-
-    def nyq_copy(level, k):
-        where = (z_peer, x_peer)[level](k)
-        return remote(nyq_out.at[level], nyq_in.at[level, k], nyq_send.at[level, k], nyq_recv.at[level, k], where)
-
-    def nyq_begin(level):
-        nyq_in[level, 0] = nyq_out[level]
-        for k in range(1, SPAN):
-            nyq_copy(level, k).start()
-
-    def nyq_collect(level):
-        for k in range(1, SPAN):
-            nyq_copy(level, k).wait_recv()
-        here = (z, x)[level]
-        total = nyq_in[level, lax.rem(here + SPAN, SPAN)]
-        for source in range(1, SPAN):
-            total = total + nyq_in[level, lax.rem(here - source + SPAN, SPAN)]
-        nyq_out[level + 1] = total
-
-    def nyq_final():
-        return remote(nyq_out.at[2], nyq_partner, nyq_core_send, nyq_core_recv, partner)
+        rows = pl.ds(pl.multiple_of(i * size, size), size)
+        fin[rows, :] = collect(x_copy, x_block, x_in, i).reshape(size, ROOT)
 
     @pl.loop(0, groups)
     def _(t):
-        side = lax.rem(t, 2)
+        side = lax.rem(t + core, 2)
         here = jnp.where(side == 0, as_int(has_right), as_int(has_left))
         load(t).wait()
         swap(t).wait_recv()
@@ -424,18 +456,48 @@
         for k in range(len(RELAYED)):
             @pl.when(jnp.logical_and(relays, t == RELAY_AT[k]))
             def _():
-                for to in range(CORES):
+                for turn in range(CORES):
+                    to = lax.rem(1 - core + turn, CORES)
                     relay_copy(k, to).wait_recv()
                     relay_on(k, to).start()
 
+        @pl.when(jnp.logical_and(crosses, t == HELD))
+        def _():
+            for turn in range(CORES):
+                halo_copy(HELD, lax.rem(core + turn, CORES)).start()
+
         def wait_halo():
+            @pl.when(t == ring_at)
+            def _():
+                @pl.loop(0, ring_at - 2)
+                def _(i):
+                    z_advance(i)
+
+            @pl.when(t >= ring_at)
+            def _():
+                z_advance(t - 2)
+
+            for at, first, last in X_START:
+                @pl.when(t == at)
+                def _():
+                    @pl.loop(first, last)
+                    def _(i):
+                        z_collect(i)
+                        begin(x_copy, i)
+
+            @pl.when(t == groups - 1)
+            def _():
+                @pl.loop(0, 4)
+                def _(i):
+                    x_advance(i)
+
             @pl.when(here == 1)
             def _():
                 halo_arrival(t // 2, side).wait_recv()
 
             @pl.when(here == 0)
             def _():
-                place = halo_place(t // 2, side)
+                place = halo_place(t // 2, side, core)
                 place[...] = jnp.zeros((ROWS, half_len), jnp.float32)
 
         nyq = group_sums(side, data.at[strip(t)], here.astype(jnp.float32), wait_halo, consts, scratch)
@@ -443,44 +505,49 @@
         for p in range(tile):
             turned = jnp.transpose(psum[p * ROOT : (p + 1) * ROOT, :])
             sums[t * tile + p] = turned.reshape(sums.shape[1:])
+
         begin(z_copy, t)
 
-        @pl.when(t >= 2)
-        def _():
-            z_advance(t - 2)
-
-        @pl.when(t >= 4)
-        def _():
-            z_collect(t - 4)
-
-    turned = jnp.transpose(nyq_rows[...])
-    nyq_out[0] = turned[:ROWS]
-    nyq_begin(0)
-    early = batches - 2
-    for b in range(early):
-        begin(x_copy, b)
-    z_advance(groups - 2)
-    z_collect(groups - 4)
-    z_collect(groups - 3)
-    begin(x_copy, early)
-    for b in range(early):
-        x_advance(b)
-    z_advance(groups - 1)
-    nyq_collect(0)
-    nyq_begin(1)
-    x_advance(early)
-    for b in range(early):
-        x_collect(b)
-    z_collect(groups - 2)
-    z_collect(groups - 1)
-    begin(x_copy, early + 1)
-    nyq_collect(1)
-    nyq_final().start()
-    x_collect(early)
-    x_advance(early + 1)
-    x_collect(early + 1)
-
-    lines = [fin[slab(i, ROWS), :] for i in range(fin.shape[0] // ROWS)]
+    nyq_box[...] = jnp.transpose(nyq_rows[...])[:ROWS]
+    direct_in[0] = nyq_box[...]
+    z_advance(10)
+    send_direct()
+    x_advance(4)
+    x_advance(5)
+    z_collect(8)
+    begin(x_copy, 8)
+    for i in range(4):
+        x_collect(i)
+    core_copy(0).start()
+    core_copy(1).start()
+    x_advance(6)
+    x_advance(7)
+    z_collect(9)
+    begin(x_copy, 9)
+    z_advance(11)
+    x_collect(4)
+    x_collect(5)
+    core_copy(2).start()
+    z_collect(10)
+    begin(x_copy, 10)
+    x_advance(8)
+    x_collect(6)
+    x_collect(7)
+    core_copy(3).start()
+    x_advance(9)
+    z_collect(11)
+    begin(x_copy, 11)
+    x_advance(10)
+    x_collect(8)
+    x_collect(9)
+    core_copy(4).start()
+    x_advance(11)
+    x_collect(10)
+    sum_direct()
+    x_collect(11)
+    core_copy(5).start()
+
+    lines = [fin[slab(i, ROWS), :] for i in range(groups * tile)]
     while len(lines) > 1:
         lines = [a + b for a, b in zip(lines[::2], lines[1::2])] + lines[len(lines) // 2 * 2 :]
     mean_out[...] = lines[0]
@@ -495,17 +562,15 @@
         mean_copy(*link).start()
     mean_in[0, 0] = mean_out[...]
 
-    nyq_final().wait_recv()
-    for source in range(CORES):
-        row = jnp.where(core == source, nyq_out[2], nyq_partner[...])
-        nyquist_ref[source : source + 1, :] = row[:1] * scale
-
     lanes = lax.broadcasted_iota(jnp.int32, (1, ROOT), 1)
 
     def unfold(both):
-        return jnp.dot(
-            both, mirror_ref[...], precision=lax.Precision.HIGHEST, preferred_element_type=jnp.float32
-        )
+        high = both.astype(jnp.bfloat16)
+        middle = (both - high.astype(jnp.float32)).astype(jnp.bfloat16)
+        rest = both - high.astype(jnp.float32) - middle.astype(jnp.float32)
+        low = rest.astype(jnp.bfloat16)
+        parts = [jnp.dot(part, mirror_ref[...], preferred_element_type=jnp.float32) for part in (low, middle, high)]
+        return parts[0] + parts[1] + parts[2]
 
     factors = [jnp.where(jnp.logical_and(lanes == 0, me + j == 0), scale, 2.0 * scale) for j in range(2)]
     pairs = mine // 2
@@ -520,38 +585,38 @@
             )
             placed = unfold(both)
             for half in range(2):
-                power_ref[pl.ds(j * CORES * mine + base + half, pairs, stride=2), :] = (
+                power_box[pl.ds(j * CORES * mine + base + half, pairs, stride=2), :] = (
                     placed[:, half * ROOT : (half + 1) * ROOT] * factors[j]
                 )
 
-    for n in range(batches):
-        for side in range(2):
-            swap(2 * n + side).wait_send()
-        core_copy(n).wait_send()
-
-        @pl.when(sends_halo)
-        def _():
-            for to in range(CORES):
-                halo_copy(n, to).wait_send()
-
-        for kind in range(3):
-            x_copy(kind, n).wait_send()
-
-    @pl.loop(0, groups)
-    def _(g):
-        for kind in range(3):
-            z_copy(kind, g).wait_send()
+    power_out = pltpu.make_async_copy(power_box, packed_ref.at[: power_box.shape[0]], out_sem.at[0])
+    power_out.start()
+
+    ends = [
+        ref[groups * size : groups * size + 1, :] * scale for ref in (fin, from_partner)
+    ]
+    parts = [jnp.where(core == source, ends[0], ends[1]) for source in range(CORES)]
+    moved = pltpu.roll(parts[1], mine, 1)
+    small_box[...] = jnp.zeros_like(small_box)
+    small_box[0:1, :] = jnp.where(lanes < mine, parts[0], moved)
+    small_box[1:2, :] = moved
+
+    def sent(box, send):
+        remote(box, box, send, core_recv.at[0], partner).wait_send()
+
+    sent(strain_ref.at[pl.ds(0, mine)], swap_send)
+    sent(z_in, z_send)
+    sent(x_in, x_send)
+    sent(fin, core_send)
+    direct_all().wait_send()
+
+    @pl.when(sends_halo)
+    def _():
+        sent(strain_ref.at[pl.ds(0, mine), pl.ds(0, half_len)], halo_send)
 
     @pl.when(relays)
     def _():
-        for k in range(len(RELAYED)):
-            for to in range(CORES):
-                relay_on(k, to).wait_send()
-
-    for level in range(2):
-        for k in range(1, SPAN):
-            nyq_copy(level, k).wait_send()
-    nyq_final().wait_send()
+        sent(relay_box, relay_send)
 
     for link in mean_links:
         mean_copy(*link).wait()
@@ -572,7 +637,20 @@
     )
     placed = placed[:, :ROOT] + placed[:, ROOT:]
     for j in range(2):
-        mean_ref[j : j + 1, :] = placed[j : j + 1] * (factors[j] * (1.0 / (CORES * mine * chan_count)))
+        small_box[2 + j : 3 + j, :] = placed[j : j + 1] * (factors[j] * (1.0 / (CORES * mine * chan_count)))
+    small_out = pltpu.make_async_copy(small_box, packed_ref.at[power_box.shape[0] :], out_sem.at[1])
+    small_out.start()
+    power_out.wait()
+    small_out.wait()
+
+
+def finish_kernel(packed_ref, power_ref, nyquist_ref, mean_ref):
+    chan_rows = power_ref.shape[0]
+    for j in range(2):
+        power_ref[:, j * ROOT : (j + 1) * ROOT] = packed_ref[j * chan_rows : (j + 1) * chan_rows, :]
+        mean_ref[:, j * ROOT : (j + 1) * ROOT] = packed_ref[2 * chan_rows + 2 + j : 2 * chan_rows + 3 + j, :]
+    nyquist_ref[:, :ROOT] = packed_ref[2 * chan_rows : 2 * chan_rows + 1, :]
+    nyquist_ref[:, ROOT:] = packed_ref[2 * chan_rows + 1 : 2 * chan_rows + 2, : chan_rows - ROOT]
 
 
 def per_device(strain):
@@ -593,27 +671,28 @@
     f32 = jnp.float32
     dma = pltpu.SemaphoreType.DMA
     relayed = len(RELAYED)
-    power, nyquist, mean_power = pl.pallas_call(
+    tables_in = (window, first_all, second_all, twist, mirror)
+    packed = pl.pallas_call(
         functools.partial(welch_kernel, 1.0 / (segments * energy)),
-        in_specs=[pl.BlockSpec(memory_space=pl.ANY)] + [vmem] * 5,
-        out_specs=[vmem] * 3,
-        out_shape=[
-            jax.ShapeDtypeStruct((2 * chan_rows, ROOT), f32),
-            jax.ShapeDtypeStruct((CORES, ROOT), f32),
-            jax.ShapeDtypeStruct((2, ROOT), f32),
-        ],
-        scratch_shapes=[
+        in_specs=[pl.BlockSpec(memory_space=pl.ANY)] * 6,
+        out_specs=pl.BlockSpec(memory_space=pl.ANY),
+        out_shape=jax.ShapeDtypeStruct((2 * chan_rows + ROWS, ROOT), f32),
+        scratch_shapes=[pltpu.VMEM(table.shape, table.dtype) for table in tables_in]
+        + [
+            pltpu.VMEM((2 * chan_rows, ROOT), f32),
+            pltpu.VMEM((ROWS, ROOT), f32),
+            dma((len(tables_in),)),
+            dma((2,)),
             pltpu.VMEM((mine, CORES * seg_len + half_len), f32),
             pltpu.VMEM((relayed, CORES, ROWS, half_len), f32),
             pltpu.VMEM((pairs, SPAN, SPAN, ROWS, ROOT), f32),
-            pltpu.VMEM((pairs * ROWS, ROOT), f32),
-            pltpu.VMEM((pairs * ROWS, ROOT), f32),
+            pltpu.VMEM(((pairs + 1) * ROWS, ROOT), f32),
+            pltpu.VMEM(((pairs + 1) * ROWS, ROOT), f32),
             pltpu.VMEM((3, groups, tile, SPAN, ROWS, ROOT), f32),
-            pltpu.VMEM((3, batches, ROWS, ROWS, ROOT), f32),
+            pltpu.VMEM((3, groups, tile, ROWS, ROOT), f32),
+            pltpu.VMEM((SPAN * SPAN, ROWS, ROOT), f32),
+            pltpu.VMEM((ROWS, ROOT), f32),
             pltpu.VMEM((ROOT, ROOT), f32),
-            pltpu.VMEM((3, ROWS, ROOT), f32),
-            pltpu.VMEM((2, SPAN, ROWS, ROOT), f32),
-            pltpu.VMEM((ROWS, ROOT), f32),
             pltpu.VMEM((ROWS * ROOT, ROOT), f32),
             pltpu.VMEM((ROWS * 2 * CORES * HALF, 4 * ROOT), jnp.bfloat16),
             pltpu.VMEM((2 * CORES * ROWS, 6 * ROOT), jnp.bfloat16),
@@ -621,22 +700,20 @@
             pltpu.VMEM((ROWS, ROOT), f32),
             pltpu.VMEM((2, chan_count, ROWS, ROOT), f32),
             dma((groups,)),
+            dma(()),
             dma((groups,)),
-            dma((groups,)),
-            dma((CORES, batches)),
+            dma(()),
             dma((2, batches)),
+            dma(()),
             dma((relayed, CORES)),
-            dma((relayed, CORES)),
+            dma(()),
             dma((3, groups)),
+            dma(()),
             dma((3, groups)),
-            dma((3, batches)),
-            dma((3, batches)),
-            dma((batches,)),
-            dma((batches,)),
-            dma((2, SPAN)),
-            dma((2, SPAN)),
             dma(()),
             dma(()),
+            dma(()),
+            dma((batches,)),
             dma((2, chan_count)),
             dma((2, chan_count)),
         ],
@@ -644,9 +721,19 @@
             collective_id=0, has_side_effects=True, vmem_limit_bytes=60 * 2**20
         ),
         name="welch",
-    )(strain, window, first_all, second_all, twist, mirror)
-    power = jnp.concatenate([power[:chan_rows], power[chan_rows:]], axis=1)
-    return (power, nyquist[:, :mine].reshape(-1), mean_power.reshape(-1))
+    )(strain, *tables_in)
+    power, nyquist, mean_power = pl.pallas_call(
+        finish_kernel,
+        in_specs=[vmem],
+        out_specs=[vmem] * 3,
+        out_shape=[
+            jax.ShapeDtypeStruct((chan_rows, 2 * ROOT), f32),
+            jax.ShapeDtypeStruct((1, chan_rows), f32),
+            jax.ShapeDtypeStruct((1, 2 * ROOT), f32),
+        ],
+        name="finish",
+    )(packed)
+    return (power, nyquist.reshape(-1), mean_power.reshape(-1))
 
 
 def solution(mesh):

time: 81.1 us -> 72.2 us (0.89)
  Pallas kernels: 75.9 us -> 71.4 us
  local copies, waits for them, and re-layouts: 3.43 us -> 0 us
    pallas_call x1, Pallas kernels: 75.9 us -> 69.8 us  [per_device(): pl.pallas_call(functools.partial(welch_kernel, 1.0 / (segments * energy))...]
    pallas_call x0 -> x1, Pallas kernels: none -> 1.62 us  [per_device(): pl.pallas_call(finish_kernel, in_specs=[vmem], out_specs=[vmem] * 3, out_...]
    reshape x1 -> x0, local copies, waits for them, and re-layouts: 1.27 us -> none  [per_device(): return (power, nyquist[:, :mine].reshape(-1), mean_power.reshape(-1))]
    unnamed x1 -> x0, local copies, waits for them, and re-layouts: 1.2 us -> none
    slice x1 -> x0, local copies, waits for them, and re-layouts: 0.95 us -> none  [per_device(): power = jnp.concatenate([power[:chan_rows], power[chan_rows:]], axis=1)]
where the time goes in v3:
time: 72.2 us; the launch traced here: 72.1 us
  Pallas kernels  71.4 us (99%)
    pallas_call x1, Pallas kernels, per_device(): pl.pallas_call(functools.partial(welch_kernel, 1.0 / (segments * energy))...  69.8 us
    pallas_call x1, Pallas kernels, per_device(): pl.pallas_call(finish_kernel, in_specs=[vmem], out_specs=[vmem] * 3, out_...  1.62 us

profile of v3, /device:TPU:1, one launch (start us, length us, event | category | flops | bytes accessed | tf_op | source)
XLA Modules:
  0.0 72.1 jit_solution(7230002949815150432)
XLA Ops:
  0.6 69.8 %welch.1.packed_ref = f32[392,128]{1,0:T(8,128)} custom-call(f32[192,16384]{1,0:T(8,128)} %strain_ref.1, f32[128,128]{1,0:T(8,128)} %constant.10.clone.window_hbm, bf16[256,256]{1,0:T(8,128)(2,1)} %constant.11.clone.first_hbm, bf16[768,256]{1,0:T(8,128)(2,1)} %constant.12.clone.second_hbm, f32[72,256]{1,0:T(8,128)} %constant.13.clone.twist_hbm, ...), custom_call_target="tpu_custom_call" | custom-call | tf_op jit(solution)/shard_map/welch/pallas_call | solution.py:675
  70.5 1.6 %finish.1 = (f32[192,256]{1,0:T(8,128)}, f32[1,192]{1,0:T(1,128)}, f32[1,256]{1,0:T(1,128)}) custom-call(f32[392,128]{1,0:T(8,128)} %welch.1.packed_ref), custom_call_target="tpu_custom_call" | custom-call | tf_op jit(solution)/shard_map/finish/pallas_call | solution.py:725

commit v4 on v3

--- a/solution.py
+++ b/solution.py
@@ -68,7 +68,8 @@
 RELAYED = (2, 4, 5)
 RELAY_AT = (2, 5, 7)
 HELD = 3
-RING_AT = (3, 7)
+LATE = ((7, 0, 4), (8, 4, 6), (9, 6, 8), (10, 8, 9), (11, 9, 10))
+SHORT = 8
 X_START = ((9, 0, 4), (10, 4, 6), (11, 6, 8))
 
 
@@ -189,7 +190,7 @@
     batches = groups // 2
     ringed = groups
     size = tile * ROWS
-    ring_at = jnp.where(jnp.logical_or(x == 0, x == SPAN - 1), RING_AT[1], RING_AT[0])
+    inner = jnp.logical_and(x > 0, x < SPAN - 1)
     has_left, has_right = chip > 0, chip < chips - 1
     exists = (has_right, has_left)
 
@@ -439,6 +440,20 @@
     def z_collect(i):
         z_block(i, 0)[...] = collect(z_copy, z_block, z_in, i)
 
+    def short_copy(k, i):
+        return remote(x_block(i, k), x_in.at[k - 1, i], x_send, x_recv.at[k - 1, i], x_peer(k))
+
+    def short_begin(i):
+        for k in (2, 1, 3):
+            short_copy(k, i).start()
+
+    def short_collect(i):
+        total = x_block(i, 0)[...]
+        for k in (1, 3, 2):
+            short_copy(k, i).wait_recv()
+            total = total + x_in[k - 1, i]
+        fin[pl.ds(i * size, size), :] = total.reshape(size, ROOT)
+
     def x_advance(i):
         advance(x_copy, x_block, x_in, i)
 
@@ -467,15 +482,16 @@
                 halo_copy(HELD, lax.rem(core + turn, CORES)).start()
 
         def wait_halo():
-            @pl.when(t == ring_at)
-            def _():
-                @pl.loop(0, ring_at - 2)
-                def _(i):
-                    z_advance(i)
-
-            @pl.when(t >= ring_at)
+            @pl.when(jnp.logical_and(inner, t >= 2))
             def _():
                 z_advance(t - 2)
+
+            for at, first, last in LATE:
+                @pl.when(jnp.logical_and(jnp.logical_not(inner), t == at))
+                def _():
+                    @pl.loop(first, last)
+                    def _(i):
+                        z_advance(i)
 
             for at, first, last in X_START:
                 @pl.when(t == at)
@@ -515,7 +531,7 @@
     x_advance(4)
     x_advance(5)
     z_collect(8)
-    begin(x_copy, 8)
+    short_begin(8)
     for i in range(4):
         x_collect(i)
     core_copy(0).start()
@@ -523,34 +539,60 @@
     x_advance(6)
     x_advance(7)
     z_collect(9)
-    begin(x_copy, 9)
+    short_begin(9)
     z_advance(11)
     x_collect(4)
     x_collect(5)
     core_copy(2).start()
     z_collect(10)
-    begin(x_copy, 10)
-    x_advance(8)
+    short_begin(10)
     x_collect(6)
     x_collect(7)
     core_copy(3).start()
-    x_advance(9)
+    short_collect(8)
+    short_collect(9)
+    core_copy(4).start()
+
+    lanes = lax.broadcasted_iota(jnp.int32, (1, ROOT), 1)
+    factors = [jnp.where(jnp.logical_and(lanes == 0, me + j == 0), scale, 2.0 * scale) for j in range(2)]
+
+    def unfold(both):
+        high = both.astype(jnp.bfloat16)
+        middle = (both - high.astype(jnp.float32)).astype(jnp.bfloat16)
+        low = (both - high.astype(jnp.float32) - middle.astype(jnp.float32)).astype(jnp.bfloat16)
+        parts = [jnp.dot(part, mirror_ref[...], preferred_element_type=jnp.float32) for part in (low, middle, high)]
+        return parts[0] + parts[1] + parts[2]
+
+    def spread(block, owner, first, count):
+        for j in range(2):
+            both = jnp.concatenate(
+                [block[pl.ds(SPAN * core + j + shift + first * ROWS, count, stride=ROWS), :] for shift in (0, 2)],
+                axis=1,
+            )
+            placed = unfold(both)
+            for half in range(2):
+                at = j * CORES * mine + owner * mine + 2 * first + half
+                power_box[pl.ds(at, count, stride=2), :] = placed[:, half * ROOT : (half + 1) * ROOT] * factors[j]
+
+    def add_tiles(first, last):
+        lines = [fin[slab(i, ROWS), :] for i in range(first, last)]
+        while len(lines) > 1:
+            lines = [a + b for a, b in zip(lines[::2], lines[1::2])] + lines[len(lines) // 2 * 2 :]
+        return lines[0]
+
+    most = 10 * tile
+    spread(fin, core, 0, most)
+    early = add_tiles(0, most)
     z_collect(11)
-    begin(x_copy, 11)
-    x_advance(10)
-    x_collect(8)
-    x_collect(9)
-    core_copy(4).start()
-    x_advance(11)
-    x_collect(10)
+    short_begin(11)
+    short_collect(10)
+    for b in range(batches - 1):
+        core_copy(b).wait_recv()
+    spread(from_partner, 1 - core, 0, most)
     sum_direct()
-    x_collect(11)
+    short_collect(11)
     core_copy(5).start()
-
-    lines = [fin[slab(i, ROWS), :] for i in range(groups * tile)]
-    while len(lines) > 1:
-        lines = [a + b for a, b in zip(lines[::2], lines[1::2])] + lines[len(lines) // 2 * 2 :]
-    mean_out[...] = lines[0]
+    mean_out[...] = early + add_tiles(most, groups * tile)
 
     def mean_copy(other, k):
         return remote(
@@ -561,34 +603,9 @@
     for link in mean_links:
         mean_copy(*link).start()
     mean_in[0, 0] = mean_out[...]
-
-    lanes = lax.broadcasted_iota(jnp.int32, (1, ROOT), 1)
-
-    def unfold(both):
-        high = both.astype(jnp.bfloat16)
-        middle = (both - high.astype(jnp.float32)).astype(jnp.bfloat16)
-        rest = both - high.astype(jnp.float32) - middle.astype(jnp.float32)
-        low = rest.astype(jnp.bfloat16)
-        parts = [jnp.dot(part, mirror_ref[...], preferred_element_type=jnp.float32) for part in (low, middle, high)]
-        return parts[0] + parts[1] + parts[2]
-
-    factors = [jnp.where(jnp.logical_and(lanes == 0, me + j == 0), scale, 2.0 * scale) for j in range(2)]
-    pairs = mine // 2
-    for which, block in enumerate((fin, from_partner)):
-        if which == 1:
-            for b in range(batches):
-                core_copy(b).wait_recv()
-        base = (core if which == 0 else 1 - core) * mine
-        for j in range(2):
-            both = jnp.concatenate(
-                [block[pl.ds(SPAN * core + j + shift, pairs, stride=ROWS), :] for shift in (0, 2)], axis=1
-            )
-            placed = unfold(both)
-            for half in range(2):
-                power_box[pl.ds(j * CORES * mine + base + half, pairs, stride=2), :] = (
-                    placed[:, half * ROOT : (half + 1) * ROOT] * factors[j]
-                )
-
+    spread(fin, core, most, groups * tile - most)
+    core_copy(batches - 1).wait_recv()
+    spread(from_partner, 1 - core, most, groups * tile - most)
     power_out = pltpu.make_async_copy(power_box, packed_ref.at[: power_box.shape[0]], out_sem.at[0])
     power_out.start()
 

time: 72.2 us -> 70.2 us (0.972)
  Pallas kernels: 71.4 us -> 69.4 us
    pallas_call x1, Pallas kernels: 69.8 us -> 67.8 us  [per_device(): pl.pallas_call(functools.partial(welch_kernel, 1.0 / (segments * energy))...]
where the time goes in v4:
time: 70.2 us; the launch traced here: 70 us
  Pallas kernels  69.4 us (99%)
    pallas_call x1, Pallas kernels, per_device(): pl.pallas_call(functools.partial(welch_kernel, 1.0 / (segments * energy))...  67.8 us
    pallas_call x1, Pallas kernels, per_device(): pl.pallas_call(finish_kernel, in_specs=[vmem], out_specs=[vmem] * 3, out_...  1.62 us

profile of v4, /device:TPU:1, one launch (start us, length us, event | category | flops | bytes accessed | tf_op | source)
XLA Modules:
  0.0 70.0 jit_solution(11116282000842810000)
XLA Ops:
  0.6 67.8 %welch.1.packed_ref = f32[392,128]{1,0:T(8,128)} custom-call(f32[192,16384]{1,0:T(8,128)} %strain_ref.1, f32[128,128]{1,0:T(8,128)} %constant.10.clone.window_hbm, bf16[256,256]{1,0:T(8,128)(2,1)} %constant.11.clone.first_hbm, bf16[768,256]{1,0:T(8,128)(2,1)} %constant.12.clone.second_hbm, f32[72,256]{1,0:T(8,128)} %constant.13.clone.twist_hbm, ...), custom_call_target="tpu_custom_call" | custom-call | tf_op jit(solution)/shard_map/welch/pallas_call | solution.py:692
  68.4 1.6 %finish.1 = (f32[192,256]{1,0:T(8,128)}, f32[1,192]{1,0:T(1,128)}, f32[1,256]{1,0:T(1,128)}) custom-call(f32[392,128]{1,0:T(8,128)} %welch.1.packed_ref), custom_call_target="tpu_custom_call" | custom-call | tf_op jit(solution)/shard_map/finish/pallas_call | solution.py:742

commit v5 on v4

--- a/solution.py
+++ b/solution.py
@@ -68,7 +68,7 @@
 RELAYED = (2, 4, 5)
 RELAY_AT = (2, 5, 7)
 HELD = 3
-LATE = ((7, 0, 4), (8, 4, 6), (9, 6, 8), (10, 8, 9), (11, 9, 10))
+LATE = ((7, 0, 4), (8, 4, 6), (9, 6, 7), (10, 7, 9), (11, 9, 10))
 SHORT = 8
 X_START = ((9, 0, 4), (10, 4, 6), (11, 6, 8))
 
@@ -171,8 +171,8 @@
 def welch_kernel(
     scale, strain_ref, window_hbm, first_hbm, second_hbm, twist_hbm, mirror_hbm, packed_ref,
     window_ref, first_ref, second_ref, twist_ref, mirror_ref, power_box, small_box, table_sem, out_sem,
-    data, relay_box, sums, fin, from_partner, z_in, x_in, direct_in, nyq_box, nyq_rows,
-    buf, zbuf, ebuf, psum, mean_out, mean_in,
+    data, relay_box, sums, fin, from_partner, z_in, x_in, direct_in, direct_out, group_sum, group_in, nyq_rows,
+    buf, zbuf, ebuf, psum,
     load_sem, swap_send, swap_recv, halo_send, halo_recv, relay_send, relay_recv,
     z_send, z_recv, x_send, x_recv, direct_send, direct_recv, core_send, core_recv, mean_send, mean_recv,
 ):
@@ -284,11 +284,8 @@
     def greet(where):
         pl.semaphore_signal(barrier, inc=1, device_id=where, device_id_type=pl.DeviceIdType.MESH)
 
-    def mean_peer(other, k):
-        where = {"chan": lax.rem(chan + k, chan_count)}
-        if other:
-            where["tm"] = chip * CORES + 1 - core
-        return where
+    def chan_peer(k):
+        return {"chan": lax.rem(chan + k, chan_count)}
 
     def chip_peer(k):
         far_z, far_x = lax.rem(z + k // SPAN, SPAN), lax.rem(x + k % SPAN, SPAN)
@@ -298,8 +295,7 @@
     for k in range(1, SPAN * SPAN):
         greet(chip_peer(k)[2])
     for k in range(1, chan_count):
-        for other in range(2):
-            greet(mean_peer(other, k))
+        greet(chan_peer(k))
     for flag, shift, both in ((has_left, -1, 0), (has_right, 1, 1)):
         @pl.when(flag)
         def _():
@@ -338,7 +334,7 @@
     right_count = as_int(has_right) * (1 + core)
     pl.semaphore_wait(
         barrier,
-        left_count + right_count + as_int(linked) + as_int(faces) + SPAN * SPAN + 2 * (chan_count - 1),
+        left_count + right_count + as_int(linked) + as_int(faces) + SPAN * SPAN + chan_count - 1,
     )
 
     for n in range(batches):
@@ -365,6 +361,7 @@
                     halo_copy(n, to).start()
 
     nyq_rows[...] = jnp.zeros_like(nyq_rows)
+    group_sum[...] = jnp.zeros_like(group_sum)
     for table in tables_in:
         table.wait()
     consts = (window_ref, first_ref, second_ref, twist_ref)
@@ -394,13 +391,13 @@
         return ring(kind, i, x_block, x_in, x_send, x_recv, x_peer)
 
     def core_copy(i):
-        count = 2 * size + (ROWS if i == batches - 1 else 0)
+        count = 2 * size + (2 * ROWS if i == batches - 1 else 0)
         rows = pl.ds(i * 2 * size, count)
         return remote(fin.at[rows], from_partner.at[rows], core_send, core_recv.at[i], partner)
 
     def direct_copy(k):
         far_z, far_x, where = chip_peer(k)
-        return remote(nyq_box, direct_in.at[k], direct_send, direct_recv, where)
+        return remote(direct_out.at[far_z, far_x], direct_in.at[k], direct_send, direct_recv, where)
 
     def direct_all():
         box = direct_in.at[pl.ds(1, SPAN * SPAN - 1)]
@@ -412,12 +409,29 @@
 
     def sum_direct():
         direct_all().wait_recv()
-        nyq = jnp.zeros((ROWS, ROOT), jnp.float32)
+        total = jnp.zeros((2, ROWS, ROOT), jnp.float32)
         for far_z in range(SPAN):
             for far_x in range(SPAN):
                 k = lax.rem(z - far_z + SPAN, SPAN) * SPAN + lax.rem(x - far_x + SPAN, SPAN)
-                nyq = nyq + direct_in[k]
-        fin[pl.ds(groups * size, ROWS), :] = nyq
+                total = total + direct_in[k]
+        fin[pl.ds(groups * size, 2 * ROWS), :] = total.reshape(2 * ROWS, ROOT)
+
+    def chan_copy(k):
+        return remote(group_sum, group_in.at[k], mean_send.at[k], mean_recv.at[k], chan_peer(k))
+
+    def chan_begin():
+        for k in (2, 1, 3):
+            chan_copy(k).start()
+        group_in[0] = group_sum[...]
+
+    def chan_collect():
+        for k in range(1, chan_count):
+            chan_copy(k).wait_recv()
+        total = group_in[lax.rem(chan + chan_count, chan_count)]
+        for source in range(1, chan_count):
+            total = total + group_in[lax.rem(chan - source + chan_count, chan_count)]
+        direct_out[:, :, 1] = total
+        direct_in[0] = direct_out[z, x]
 
     def begin(copy, i):
         copy(0, i).start()
@@ -518,34 +532,42 @@
 
         nyq = group_sums(side, data.at[strip(t)], here.astype(jnp.float32), wait_halo, consts, scratch)
         nyq_rows[strip(t), :] = jnp.broadcast_to(nyq, (ROWS, ROOT))
+        added = group_sum[...]
         for p in range(tile):
-            turned = jnp.transpose(psum[p * ROOT : (p + 1) * ROOT, :])
-            sums[t * tile + p] = turned.reshape(sums.shape[1:])
+            turned = jnp.transpose(psum[p * ROOT : (p + 1) * ROOT, :]).reshape(sums.shape[1:])
+            sums[t * tile + p] = turned
+            added = added + turned
+        group_sum[...] = added
 
         begin(z_copy, t)
 
-    nyq_box[...] = jnp.transpose(nyq_rows[...])[:ROWS]
-    direct_in[0] = nyq_box[...]
+    chan_begin()
+    direct_out[:, :, 0] = jnp.broadcast_to(
+        jnp.transpose(nyq_rows[...])[:ROWS].reshape(1, 1, ROWS, ROOT), (SPAN, SPAN, ROWS, ROOT)
+    )
     z_advance(10)
-    send_direct()
     x_advance(4)
     x_advance(5)
     z_collect(8)
     short_begin(8)
+    z_collect(9)
+    short_begin(9)
+    x_advance(6)
+    x_advance(7)
+    z_advance(11)
+    z_collect(10)
+    short_begin(10)
+    chan_collect()
+    send_direct()
     for i in range(4):
         x_collect(i)
     core_copy(0).start()
     core_copy(1).start()
-    x_advance(6)
-    x_advance(7)
-    z_collect(9)
-    short_begin(9)
-    z_advance(11)
+    z_collect(11)
+    short_begin(11)
     x_collect(4)
     x_collect(5)
     core_copy(2).start()
-    z_collect(10)
-    short_begin(10)
     x_collect(6)
     x_collect(7)
     core_copy(3).start()
@@ -574,17 +596,8 @@
                 at = j * CORES * mine + owner * mine + 2 * first + half
                 power_box[pl.ds(at, count, stride=2), :] = placed[:, half * ROOT : (half + 1) * ROOT] * factors[j]
 
-    def add_tiles(first, last):
-        lines = [fin[slab(i, ROWS), :] for i in range(first, last)]
-        while len(lines) > 1:
-            lines = [a + b for a, b in zip(lines[::2], lines[1::2])] + lines[len(lines) // 2 * 2 :]
-        return lines[0]
-
     most = 10 * tile
     spread(fin, core, 0, most)
-    early = add_tiles(0, most)
-    z_collect(11)
-    short_begin(11)
     short_collect(10)
     for b in range(batches - 1):
         core_copy(b).wait_recv()
@@ -592,59 +605,23 @@
     sum_direct()
     short_collect(11)
     core_copy(5).start()
-    mean_out[...] = early + add_tiles(most, groups * tile)
-
-    def mean_copy(other, k):
-        return remote(
-            mean_out, mean_in.at[other, k], mean_send.at[other, k], mean_recv.at[other, k], mean_peer(other, k)
-        )
-
-    mean_links = [(other, k) for other in range(2) for k in range(chan_count) if other + k > 0]
-    for link in mean_links:
-        mean_copy(*link).start()
-    mean_in[0, 0] = mean_out[...]
     spread(fin, core, most, groups * tile - most)
     core_copy(batches - 1).wait_recv()
     spread(from_partner, 1 - core, most, groups * tile - most)
     power_out = pltpu.make_async_copy(power_box, packed_ref.at[: power_box.shape[0]], out_sem.at[0])
     power_out.start()
 
-    ends = [
-        ref[groups * size : groups * size + 1, :] * scale for ref in (fin, from_partner)
-    ]
+    ends = [ref[groups * size : groups * size + 1, :] * scale for ref in (fin, from_partner)]
     parts = [jnp.where(core == source, ends[0], ends[1]) for source in range(CORES)]
     moved = pltpu.roll(parts[1], mine, 1)
     small_box[...] = jnp.zeros_like(small_box)
     small_box[0:1, :] = jnp.where(lanes < mine, parts[0], moved)
     small_box[1:2, :] = moved
-
-    def sent(box, send):
-        remote(box, box, send, core_recv.at[0], partner).wait_send()
-
-    sent(strain_ref.at[pl.ds(0, mine)], swap_send)
-    sent(z_in, z_send)
-    sent(x_in, x_send)
-    sent(fin, core_send)
-    direct_all().wait_send()
-
-    @pl.when(sends_halo)
-    def _():
-        sent(strain_ref.at[pl.ds(0, mine), pl.ds(0, half_len)], halo_send)
-
-    @pl.when(relays)
-    def _():
-        sent(relay_box, relay_send)
-
-    for link in mean_links:
-        mean_copy(*link).wait()
-    total = jnp.zeros((ROWS, ROOT), jnp.float32)
-    for source_chan in range(chan_count):
-        for source_core in range(CORES):
-            total = total + mean_in[
-                lax.rem(core + source_core, CORES), lax.rem(chan - source_chan + chan_count, chan_count)
-            ]
-    mean_out[...] = total
-    rows = [mean_out[pl.ds(SPAN * core + j, 1), :] for j in range(SPAN)]
+    rows = []
+    for j in range(SPAN):
+        at = pl.ds(groups * size + ROWS + SPAN * core + j, 1)
+        here, there = fin[at, :], from_partner[at, :]
+        rows.append(jnp.where(core == 0, here, there) + jnp.where(core == 0, there, here))
     placed = unfold(
         jnp.concatenate(
             [jnp.concatenate([rows[j], rows[j + 2]], axis=1) for j in range(2)]
@@ -657,6 +634,26 @@
         small_box[2 + j : 3 + j, :] = placed[j : j + 1] * (factors[j] * (1.0 / (CORES * mine * chan_count)))
     small_out = pltpu.make_async_copy(small_box, packed_ref.at[power_box.shape[0] :], out_sem.at[1])
     small_out.start()
+
+    def sent(box, send):
+        remote(box, box, send, core_recv.at[0], partner).wait_send()
+
+    sent(strain_ref.at[pl.ds(0, mine)], swap_send)
+    sent(z_in, z_send)
+    sent(x_in, x_send)
+    sent(fin, core_send)
+    direct_all().wait_send()
+
+    @pl.when(sends_halo)
+    def _():
+        sent(strain_ref.at[pl.ds(0, mine), pl.ds(0, half_len)], halo_send)
+
+    @pl.when(relays)
+    def _():
+        sent(relay_box, relay_send)
+
+    for k in range(1, chan_count):
+        chan_copy(k).wait_send()
     power_out.wait()
     small_out.wait()
 
@@ -703,19 +700,19 @@
             pltpu.VMEM((mine, CORES * seg_len + half_len), f32),
             pltpu.VMEM((relayed, CORES, ROWS, half_len), f32),
             pltpu.VMEM((pairs, SPAN, SPAN, ROWS, ROOT), f32),
-            pltpu.VMEM(((pairs + 1) * ROWS, ROOT), f32),
-            pltpu.VMEM(((pairs + 1) * ROWS, ROOT), f32),
+            pltpu.VMEM(((pairs + 2) * ROWS, ROOT), f32),
+            pltpu.VMEM(((pairs + 2) * ROWS, ROOT), f32),
             pltpu.VMEM((3, groups, tile, SPAN, ROWS, ROOT), f32),
             pltpu.VMEM((3, groups, tile, ROWS, ROOT), f32),
-            pltpu.VMEM((SPAN * SPAN, ROWS, ROOT), f32),
-            pltpu.VMEM((ROWS, ROOT), f32),
+            pltpu.VMEM((SPAN * SPAN, 2, ROWS, ROOT), f32),
+            pltpu.VMEM((SPAN, SPAN, 2, ROWS, ROOT), f32),
+            pltpu.VMEM((SPAN, SPAN, ROWS, ROOT), f32),
+            pltpu.VMEM((chan_count, SPAN, SPAN, ROWS, ROOT), f32),
             pltpu.VMEM((ROOT, ROOT), f32),
             pltpu.VMEM((ROWS * ROOT, ROOT), f32),
             pltpu.VMEM((ROWS * 2 * CORES * HALF, 4 * ROOT), jnp.bfloat16),
             pltpu.VMEM((2 * CORES * ROWS, 6 * ROOT), jnp.bfloat16),
             pltpu.VMEM((ROWS * HALF, ROOT), f32),
-            pltpu.VMEM((ROWS, ROOT), f32),
-            pltpu.VMEM((2, chan_count, ROWS, ROOT), f32),
             dma((groups,)),
             dma(()),
             dma((groups,)),
@@ -731,8 +728,8 @@
             dma(()),
             dma(()),
             dma((batches,)),
-            dma((2, chan_count)),
-            dma((2, chan_count)),
+            dma((chan_count,)),
+            dma((chan_count,)),
         ],
         compiler_params=pltpu.CompilerParams(
             collective_id=0, has_side_effects=True, vmem_limit_bytes=60 * 2**20

time: 70.2 us -> 67.9 us (0.967)
  Pallas kernels: 69.4 us -> 67.2 us
    pallas_call x1, Pallas kernels: 67.8 us -> 65.5 us  [per_device(): pl.pallas_call(functools.partial(welch_kernel, 1.0 / (segments * energy))...]
where the time goes in v5:
time: 67.9 us; the launch traced here: 67.8 us
  Pallas kernels  67.2 us (99%)
    pallas_call x1, Pallas kernels, per_device(): pl.pallas_call(functools.partial(welch_kernel, 1.0 / (segments * energy))...  65.5 us
    pallas_call x1, Pallas kernels, per_device(): pl.pallas_call(finish_kernel, in_specs=[vmem], out_specs=[vmem] * 3, out_...  1.62 us

profile of v5, /device:TPU:1, one launch (start us, length us, event | category | flops | bytes accessed | tf_op | source)
XLA Modules:
  0.0 67.8 jit_solution(13196012699704401364)
XLA Ops:
  0.6 65.5 %welch.1.packed_ref = f32[392,128]{1,0:T(8,128)} custom-call(f32[192,16384]{1,0:T(8,128)} %strain_ref.1, f32[128,128]{1,0:T(8,128)} %constant.10.clone.window_hbm, bf16[256,256]{1,0:T(8,128)(2,1)} %constant.11.clone.first_hbm, bf16[768,256]{1,0:T(8,128)(2,1)} %constant.12.clone.second_hbm, f32[72,256]{1,0:T(8,128)} %constant.13.clone.twist_hbm, ...), custom_call_target="tpu_custom_call" | custom-call | tf_op jit(solution)/shard_map/welch/pallas_call | solution.py:689
  66.2 1.6 %finish.1 = (f32[192,256]{1,0:T(8,128)}, f32[1,192]{1,0:T(1,128)}, f32[1,256]{1,0:T(1,128)}) custom-call(f32[392,128]{1,0:T(8,128)} %welch.1.packed_ref), custom_call_target="tpu_custom_call" | custom-call | tf_op jit(solution)/shard_map/finish/pallas_call | solution.py:739

commit v6 on v5

--- a/solution.py
+++ b/solution.py
@@ -68,6 +68,7 @@
 RELAYED = (2, 4, 5)
 RELAY_AT = (2, 5, 7)
 HELD = 3
+CHUNK = 4
 LATE = ((7, 0, 4), (8, 4, 6), (9, 6, 7), (10, 7, 9), (11, 9, 10))
 SHORT = 8
 X_START = ((9, 0, 4), (10, 4, 6), (11, 6, 8))
@@ -80,14 +81,15 @@
     return jnp.sum(parts[0], axis=1, keepdims=True)
 
 
-def stage_one(piece, mean, consts, buf, zbuf, ebuf, seg, segs):
-    window_ref, first_ref, _, twist_ref = consts
+def window_piece(piece, mean, consts, buf, ebuf, seg):
+    window_ref, _, _, twist_ref = consts
+    base = (seg % 2) * ROWS * ROOT
     mean = jnp.broadcast_to(mean, (ROWS, ROOT))
     even = jnp.zeros((ROWS, ROOT), jnp.float32)
     odd = jnp.zeros((ROWS, ROOT), jnp.float32)
     for a in range(ROOT):
         tile = (piece[:, ROOT * a : ROOT * (a + 1)] - mean) * window_ref[a : a + 1, :]
-        buf[ROWS * a : ROWS * (a + 1), :] = tile
+        buf[base + ROWS * a : base + ROWS * (a + 1), :] = tile
         if a % 2 == 0:
             even = even + tile
         else:
@@ -98,31 +100,44 @@
     turn = twist_ref[HALF : HALF + 1, :]
     high, low = split(jnp.concatenate([alt * turn[:, :ROOT], -alt * turn[:, ROOT:]], axis=1))
     ebuf[seg * ROWS : (seg + 1) * ROWS, :] = jnp.concatenate([high, low, high], axis=1)
+    return edge * edge
+
+
+def stage_one(seg, r, consts, buf, zbuf):
+    _, first_ref, _, twist_ref = consts
+    base = (seg % 2) * ROWS * ROOT
     cos_t, sin_t = twist_ref[:HALF, :ROOT], twist_ref[:HALF, ROOT:]
-    for r in range(0, ROWS, 2):
-        pair = jnp.concatenate(
-            [buf[pl.ds(r, ROOT, stride=ROWS), :], buf[pl.ds(r + 1, ROOT, stride=ROWS), :]], axis=1
+    pair = jnp.concatenate(
+        [buf[pl.ds(base + r + s, ROOT, stride=ROWS), :] for s in range(2)], axis=1
+    )
+    high, low = split(pair)
+    right = jnp.concatenate([high, low], axis=0)
+    out = jnp.dot(first_ref[:ROOT, :], right, preferred_element_type=jnp.float32)
+    out = out + jnp.dot(first_ref[ROOT:, :], right, preferred_element_type=jnp.float32)
+    for s in range(2):
+        re = out[:HALF, s * ROOT : (s + 1) * ROOT]
+        im = out[HALF:, s * ROOT : (s + 1) * ROOT]
+        z_hi, z_lo = split(
+            jnp.concatenate([re * cos_t + im * sin_t, im * cos_t - re * sin_t], axis=1)
         )
-        high, low = split(pair)
-        out = jnp.dot(
-            first_ref[...], jnp.concatenate([high, low], axis=0), preferred_element_type=jnp.float32
-        )
-        out = out[:ROOT] + out[ROOT:]
-        for s in range(2):
-            re = out[:HALF, s * ROOT : (s + 1) * ROOT]
-            im = out[HALF:, s * ROOT : (s + 1) * ROOT]
-            z_hi, z_lo = split(
-                jnp.concatenate([re * cos_t + im * sin_t, im * cos_t - re * sin_t], axis=1)
-            )
-            at = ((r + s) * segs + seg) * HALF
-            zbuf[at : at + HALF, 0 : 2 * ROOT] = z_hi
-            zbuf[at : at + HALF, 2 * ROOT :] = z_lo
-    return edge * edge
+        at = (seg * ROWS + r + s) * HALF
+        zbuf[at : at + HALF, 0 : 2 * ROOT] = z_hi
+        zbuf[at : at + HALF, 2 * ROOT :] = z_lo
 
 
 def squares(left, right):
     out = jnp.dot(left, right, preferred_element_type=jnp.float32)
     return out[:, :ROOT] * out[:, :ROOT] + out[:, ROOT:] * out[:, ROOT:]
+
+
+def stage_two(seg, r, count, weight, consts, zbuf, psum):
+    at = slice((seg * ROWS + r) * HALF, (seg * ROWS + r + count) * HALF)
+    left = jnp.concatenate([zbuf[at, :], zbuf[at, : 2 * ROOT]], axis=1)
+    power = squares(left, consts[2][...])
+    if weight is not None:
+        power = weight * power
+    to = slice(r * HALF, (r + count) * HALF)
+    psum[to, :] = power if seg == 0 else psum[to, :] + power
 
 
 def group_sums(side, rows, on, wait_halo, consts, scratch):
@@ -140,29 +155,32 @@
     inverse = 1.0 / (2 * half_len)
     nyq = jnp.zeros((ROWS, 1), jnp.float32)
     for seg in range(segs - 1):
-        nyq = nyq + stage_one(
+        nyq = nyq + window_piece(
             window(own + seg * half_len, 2 * half_len), (totals[seg] + totals[seg + 1]) * inverse,
-            consts, buf, zbuf, ebuf, seg, segs,
+            consts, buf, ebuf, seg,
         )
+        for r in range(0, ROWS, 2):
+            stage_one(seg, r, consts, buf, zbuf)
+            if seg > 0 and (r + 2) % CHUNK == 0:
+                stage_two(seg - 1, r + 2 - CHUNK, CHUNK, None, consts, zbuf, psum)
     wait_halo()
+    last = segs - 1
     near = jnp.where(side == 0, totals[-1], totals[0])
     far = half_sum(window((1 - side) * segs * half_len, half_len))
-    nyq = nyq + on * stage_one(
-        window((1 - side) * (segs - 1) * half_len, 2 * half_len), (near + far) * inverse,
-        consts, buf, zbuf, ebuf, segs - 1, segs,
+    nyq = nyq + on * window_piece(
+        window((1 - side) * last * half_len, 2 * half_len), (near + far) * inverse, consts, buf, ebuf, last
     )
-
-    def fold(power, count):
-        total = power[:count]
-        for seg in range(1, segs - 1):
-            total = total + power[seg * count : (seg + 1) * count]
-        return total + on * power[(segs - 1) * count :]
-
-    for r in range(ROWS):
-        at = slice(r * segs * HALF, (r + 1) * segs * HALF)
-        left = jnp.concatenate([zbuf[at, :], zbuf[at, : 2 * ROOT]], axis=1)
-        psum[r * HALF : (r + 1) * HALF, :] = fold(squares(left, second_ref[...]), HALF)
-    mixed = fold(squares(ebuf[...], second_ref[...]), ROWS)
+    for r in range(0, ROWS, 2):
+        stage_one(last, r, consts, buf, zbuf)
+        if (r + 2) % CHUNK == 0:
+            stage_two(last - 1, r + 2 - CHUNK, CHUNK, None, consts, zbuf, psum)
+    for r in range(0, ROWS, CHUNK):
+        stage_two(last, r, CHUNK, on, consts, zbuf, psum)
+    power = squares(ebuf[...], second_ref[...])
+    mixed = power[:ROWS]
+    for seg in range(1, last):
+        mixed = mixed + power[seg * ROWS : (seg + 1) * ROWS]
+    mixed = mixed + on * power[last * ROWS :]
     first_rows = pl.ds(0, ROWS, stride=HALF)
     psum[first_rows, :] = jnp.where(lane % SPAN >= SPAN // 2, mixed, psum[first_rows, :])
     return nyq
@@ -709,7 +727,7 @@
             pltpu.VMEM((SPAN, SPAN, ROWS, ROOT), f32),
             pltpu.VMEM((chan_count, SPAN, SPAN, ROWS, ROOT), f32),
             pltpu.VMEM((ROOT, ROOT), f32),
-            pltpu.VMEM((ROWS * ROOT, ROOT), f32),
+            pltpu.VMEM((2 * ROWS * ROOT, ROOT), f32),
             pltpu.VMEM((ROWS * 2 * CORES * HALF, 4 * ROOT), jnp.bfloat16),
             pltpu.VMEM((2 * CORES * ROWS, 6 * ROOT), jnp.bfloat16),
             pltpu.VMEM((ROWS * HALF, ROOT), f32),

time: 67.9 us -> 66.3 us (0.976)
  Pallas kernels: 67.2 us -> 65.5 us
    pallas_call x1, Pallas kernels: 65.5 us -> 63.9 us  [per_device(): pl.pallas_call(functools.partial(welch_kernel, 1.0 / (segments * energy))...]
where the time goes in v6:
time: 66.3 us; the launch traced here: 66.2 us
  Pallas kernels  65.5 us (99%)
    pallas_call x1, Pallas kernels, per_device(): pl.pallas_call(functools.partial(welch_kernel, 1.0 / (segments * energy))...  63.9 us
    pallas_call x1, Pallas kernels, per_device(): pl.pallas_call(finish_kernel, in_specs=[vmem], out_specs=[vmem] * 3, out_...  1.62 us

profile of v6, /device:TPU:1, one launch (start us, length us, event | category | flops | bytes accessed | tf_op | source)
XLA Modules:
  0.0 66.2 jit_solution(8386929408921843669)
XLA Ops:
  0.6 63.9 %welch.1.packed_ref = f32[392,128]{1,0:T(8,128)} custom-call(f32[192,16384]{1,0:T(8,128)} %strain_ref.1, f32[128,128]{1,0:T(8,128)} %constant.10.clone.window_hbm, bf16[256,256]{1,0:T(8,128)(2,1)} %constant.11.clone.first_hbm, bf16[768,256]{1,0:T(8,128)(2,1)} %constant.12.clone.second_hbm, f32[72,256]{1,0:T(8,128)} %constant.13.clone.twist_hbm, ...), custom_call_target="tpu_custom_call" | custom-call | tf_op jit(solution)/shard_map/welch/pallas_call | solution.py:707
  64.5 1.6 %finish.1 = (f32[192,256]{1,0:T(8,128)}, f32[1,192]{1,0:T(1,128)}, f32[1,256]{1,0:T(1,128)}) custom-call(f32[392,128]{1,0:T(8,128)} %welch.1.packed_ref), custom_call_target="tpu_custom_call" | custom-call | tf_op jit(solution)/shard_map/finish/pallas_call | solution.py:757
